TPU v7x, 128 devices: a whole 4x4x4 slice. The times are simulated.
128 devices in a mesh: model: 4 (over x), data: 32 (over z, y, core).
Axes of the slice: x: 4, y: 4, z: 4, core: 2. Of those that a mesh axis runs over, the one named last changes fastest.
Arguments:
- local_grads: bfloat16 [32, 24, 589824], P('data', None, 'model')
- master: float32 [24, 589824], P(None, ('model', 'data'))
- moment_one: float32 [24, 589824], P(None, ('model', 'data'))
- moment_two: float32 [24, 589824], P(None, ('model', 'data'))
Outputs:
- output 1: bfloat16 [24, 589824], P(None, 'model')
- output 2: float32 [24, 589824], P(None, ('model', 'data'))
- output 3: float32 [24, 589824], P(None, ('model', 'data'))
- output 4: float32 [24, 589824], P(None, ('model', 'data'))
All inputs are finite; a program needn't handle non-finite values.
Results may differ from a plain program's by a relative error of at most 0.001.
Values are sent between devices in bfloat16 or wider.
A program may use at most 1 GiB of HBM per device.

v0:
```python
import jax
import jax.numpy as jnp
from jax import lax
from jax.sharding import PartitionSpec as P

STEP = 4
LEARN_RATE = 0.08
BETA_ONE = 0.9
BETA_TWO = 0.999
EPSILON = 1e-6
WEIGHT_DECAY = 0.01
MAX_NORM = 1.0
CORR_ONE = 1.0 - BETA_ONE ** STEP
CORR_TWO = 1.0 - BETA_TWO ** STEP


def tensor_sums(block_values):
    return jnp.stack([block_values[..., 0:3].sum(axis=-1), block_values[..., 3], block_values[..., 4:8].sum(axis=-1), block_values[..., 8:12].sum(axis=-1)], axis=-1)


def spread_tensors(tensor_values):
    lead_shape = tensor_values.shape[:-1]
    pieces = [jnp.broadcast_to(tensor_values[..., tensor_pos:tensor_pos + 1], lead_shape + (block_count,)) for tensor_pos, block_count in enumerate((3, 1, 4, 4))]
    return jnp.concatenate(pieces, axis=-1)


def adam_direction(grad_mean, clip_scale, master, moment_one, moment_two):
    scaled = clip_scale * grad_mean
    new_one = BETA_ONE * moment_one + (1.0 - BETA_ONE) * scaled
    new_two = BETA_TWO * moment_two + (1.0 - BETA_TWO) * scaled * scaled
    direction = (new_one / CORR_ONE) / (jnp.sqrt(new_two / CORR_TWO) + EPSILON) + WEIGHT_DECAY * master
    return new_one, new_two, direction


def block_ratio(norm_sq):
    tensor_norms = jnp.sqrt(tensor_sums(norm_sq.reshape(2, -1, 12)))
    return spread_tensors(tensor_norms[0] / tensor_norms[1]).reshape(-1, 1)


def solution(mesh):
    data_size = mesh.shape['data']
    both_axes = ('model', 'data')
    state_spec = P(None, both_axes)

    def device_step(local_grads, master, moment_one, moment_two):
        grad_slab = local_grads[0]
        received = lax.all_to_all(grad_slab, 'data', 1, 0, tiled=True)
        grad_mean = jnp.sum(received.reshape(data_size, grad_slab.shape[0], -1), axis=0, dtype=jnp.float32) / data_size
        total_sq = lax.psum(jnp.sum(grad_mean * grad_mean), both_axes)
        clip_scale = jnp.minimum(1.0, MAX_NORM / jnp.sqrt(total_sq))
        new_one, new_two, direction = adam_direction(grad_mean, clip_scale, master, moment_one, moment_two)
        norm_sq = lax.psum(jnp.stack([jnp.sum(master * master, axis=1), jnp.sum(direction * direction, axis=1)]), both_axes)
        new_master = master - LEARN_RATE * block_ratio(norm_sq) * direction
        params = lax.all_gather(new_master.astype(jnp.bfloat16), 'data', axis=1, tiled=True)
        return params, new_master, new_one, new_two

    return jax.shard_map(device_step, mesh=mesh, in_specs=(P('data', None, 'model'), state_spec, state_spec, state_spec), out_specs=(P(None, 'model'), state_spec, state_spec, state_spec), check_vma=False)
```

profile of v0, /device:TPU:1, one launch (start us, length us, event | category | flops | bytes accessed | tf_op | source)
XLA Modules:
  0.0 308.6 jit_solution(6604456342513114480)
XLA Ops:
  7.2 0.0 all-gather.2.cloned.1.call-start
  7.2 5.2 %copy.21 = bf16[3,8,32,4608]{3,2,1,0:T(8,128)(2,1)S(1)} copy(bf16[3,8,32,4608]{3,1,2,0:T(8,128)(2,1)} %bitcast.11) | data formatting | bytes 14155776
  12.4 3.9 %copy.17 = bf16[24,32,4608]{2,0,1:T(8,128)(2,1)S(1)} copy(bf16[24,32,4608]{2,1,0:T(8,128)(2,1)S(1)} %bitcast.10) | data formatting | bytes 14155776 | tf_op jit(solution)/shard_map/all_to_all | solution.py:47
  16.3 96.6 %all_to_all.13 = bf16[24,32,4608]{2,0,1:T(8,128)(2,1)S(1)} all-to-all(bf16[24,32,4608]{2,0,1:T(8,128)(2,1)S(1)} %copy.17), channel_id=1, replica_groups=mesh['model'=4,'data'=32] {'data'}, dimensions={1} | all-to-all | bytes 14155776 | tf_op jit(solution)/shard_map/all_to_all | solution.py:47
  112.9 1.2 convert_reduce_fusion
  114.1 0.7 multiply_reduce_fusion.1
  114.8 65.9 %psum.14 = f32[]{:T(128)} all-reduce(f32[]{:T(128)} %multiply_reduce_fusion.1), channel_id=1, replica_groups=mesh['model'=4,'data'=32] {'model','data'}, use_global_device_ids=true, to_apply=%region_3.0 | all-reduce | flops 1 | bytes 8 | tf_op jit(solution)/shard_map/psum | solution.py:49
  181.4 0.0 copy-done
  181.4 0.0 copy-done.3
  181.4 0.6 multiply_reduce_fusion.2
  182.0 0.0 copy-start.1
  182.0 0.0 copy-start.2
  182.0 0.1 reshape.28
  182.1 62.5 %psum.15 = f32[2,2,12]{2,1,0:T(2,128)S(1)} all-reduce(f32[2,2,12]{2,1,0:T(2,128)S(1)} %reshape.28), channel_id=1, replica_groups=mesh['model'=4,'data'=32] {'model','data'}, use_global_device_ids=true, to_apply=%region_5.0 | all-reduce | flops 48 | bytes 384 | tf_op jit(solution)/shard_map/psum | solution.py:52
  244.5 0.1 slice_reduce_fusion.2
  244.6 0.1 slice.41
  244.7 0.2 slice_reduce_fusion.1
  244.9 0.1 copy.18
  245.0 0.1 copy.20
  245.1 0.1 copy.19
  245.2 0.1 maximum_sqrt_fusion
  245.3 0.2 slice_reduce_fusion.5
  245.5 0.1 broadcast_in_dim.22
  245.5 0.1 broadcast_in_dim.26
  245.6 0.1 broadcast_in_dim.24
  245.7 0.1 maximum_multiply_fusion
  245.7 0.1 mul.87
  245.8 1.1 fusion.2
  246.9 0.0 all-gather.2.cloned.1.call-update
  247.0 47.9 %all-gather.2.cloned.1.call-done = bf16[24,147456]{1,0:T(8,128)(2,1)} async-done(((bf16[24,4608]{1,0:T(8,128)(2,1)}), bf16[24,147456]{1,0:T(8,128)(2,1)}) %all-gather.2.cloned.1.call-update) | async-done | bytes 7077904 | tf_op jit(solution)/shard_map/all_gather | solution.py:54
  294.9 6.9 %copy.23 = bf16[24,147456]{1,0:T(8,128)(2,1)} copy(bf16[24,147456]{1,0:T(8,128)(2,1)} %all-gather.2.cloned.1.call-done) | data formatting | bytes 14155776
  301.8 0.0 copy-done.1
  (7 shorter events, 0.0 us)
Async XLA Ops:
  7.2 287.7 %all-gather.2.cloned.1.call-start = ((), (), s32[]{:S(2)}) async-start(), calls=%async_computation.1 | async-start | bytes 7299072 | tf_op jit(solution)/shard_map/all_gather | solution.py:54
  112.9 68.5 %copy-start = (f32[24,4608]{1,0:T(8,128)S(1)}, f32[24,4608]{1,0:T(8,128)}, u32[]{:S(2)}) copy-start(f32[24,4608]{1,0:T(8,128)} %param.5) | copy-start | bytes 1327108
  112.9 68.5 %copy-start.3 = (f32[24,4608]{1,0:T(8,128)S(1)}, f32[24,4608]{1,0:T(8,128)}, u32[]{:S(2)}) copy-start(f32[24,4608]{1,0:T(8,128)} %param.6) | copy-start | bytes 1327108
  112.9 68.5 %copy-start.4 = (f32[24,4608]{1,0:T(8,128)S(1)}, f32[24,4608]{1,0:T(8,128)}, u32[]{:S(2)}) copy-start(f32[24,4608]{1,0:T(8,128)} %param.7) | copy-start | bytes 1327108
  182.0 119.8 %copy-start.1 = (f32[24,4608]{1,0:T(8,128)}, f32[24,4608]{1,0:T(8,128)S(1)}, u32[]{:S(2)}) copy-start(f32[24,4608]{1,0:T(8,128)S(1)} %get-tuple-element.22) | copy-start | bytes 1327108
  182.0 119.8 %copy-start.2 = (f32[24,4608]{1,0:T(8,128)}, f32[24,4608]{1,0:T(8,128)S(1)}, u32[]{:S(2)}) copy-start(f32[24,4608]{1,0:T(8,128)S(1)} %get-tuple-element.23) | copy-start | bytes 1327108
Sparse Core Ops, SparseCore 0:
  247.1 47.7 all-gather.1
where the time goes:
time: 309 us
  blocking collectives  225 us (73%)
  waiting for transfers between devices  48 us (16%)
  local copies, waits for them, and re-layouts  16.9 us (5%)
  between operations  14.8 us (5%)
  other arithmetic  4.01 us (1%)
    all_to_all x1, blocking collectives, device_step(): received = lax.all_to_all(grad_slab, 'data', 1, 0, tiled=True)  96.6 us
    psum x1, blocking collectives, device_step(): total_sq = lax.psum(jnp.sum(grad_mean * grad_mean), both_axes)  65.9 us
    psum x1, blocking collectives, device_step(): lax.psum(jnp.stack([jnp.sum(master * master, axis=1), jnp.sum(direction *...  62.5 us
    all_gather x1, waiting for transfers between devices, device_step(): lax.all_gather(new_master.astype(jnp.bfloat16), 'data', axis=1, tiled=True)  47.9 us
    unnamed x12, local copies, waits for them, and re-layouts  12.1 us
  transfers between devices with their start and end apart: 1, of which 1 were waited for; matrix products, arithmetic and copies ran while one was open for 0% of the time, Pallas kernels for 0%

commit v1 on v0

v1 whole, which is shorter than its diff:
```python
import functools

import jax
import jax.numpy as jnp
from jax import lax
from jax.experimental import pallas as pl
from jax.experimental.pallas import tpu as pltpu
from jax.sharding import PartitionSpec as P

STEP = 4
LEARN_RATE = 0.08
BETA_ONE = 0.9
BETA_TWO = 0.999
EPSILON = 1e-6
WEIGHT_DECAY = 0.01
MAX_NORM = 1.0
CORR_ONE = 1.0 - BETA_ONE ** STEP
CORR_TWO = 1.0 - BETA_TWO ** STEP

MESH = pl.DeviceIdType.MESH
TILES = 3
SLAB = 4608
HALF = SLAB // 2
STEP_COLS = 768
REPLICAS = 32
PLUS_SET = (2, 0)
MINUS_SET = (3, 1)
SUM_ROUNDS = (
    tuple((0, 0, k, 0) for k in (1, 2, 3)),
    tuple((0, k, 0, 0) for k in (1, 2, 3)),
    tuple((k, 0, 0, e) for k in (0, 1, 2, 3) for e in (0, 1) if (k, e) != (0, 0)),
)
SLOTS = max(len(group) for group in SUM_ROUNDS)
COPIES = 120
LOADS = 18


def lamb_kernel(grads, master_in, one_in, two_in, params, master_out, one_out, two_out, own_raw, pair_raw, relay_raw, early, late, fin, sums, mid, end, master, one, two, grad_sum, direction, tiles, slots, send_sem, recv_sem, load_sem):
    x, data = lax.axis_index('model'), lax.axis_index('data')
    core, y, z = lax.rem(data, 2), lax.rem(data // 2, 4), data // 8
    started = []
    loads = []

    def peer(dx, dz, dy, dc):
        chip = lax.rem(z + dz + 4, 4) * 4 + lax.rem(y + dy + 4, 4)
        return lax.rem(x + dx, 4), chip * 2 + lax.rem(core + dc, 2)

    def ring_a(step, other=0):
        role = core if not other else 1 - core
        return peer(0, step * role, step * (1 - role), other)

    def ring_b(step):
        return peer(0, step * (1 - core), step * core, 0)

    def column(da, db, other=0):
        role = core if not other else 1 - core
        dy, dz = da * (1 - role) + db * role, da * role + db * (1 - role)
        slab = (lax.rem(z + dz + 4, 4) * 4 + lax.rem(y + dy + 4, 4)) * 2 + role
        return pl.multiple_of(slab * SLAB, SLAB)

    def slab_of(ref, da, db, other=0):
        return ref.at[:, :, pl.ds(column(da, db, other), SLAB)]

    def half_of(ref, da, db, half):
        return ref.at[:, :, pl.ds(pl.multiple_of(column(da, db) + half * HALF, HALF), HALF)]

    def remote(src, dst, device):
        index = len(started)
        copy = pltpu.make_async_remote_copy(src_ref=src, dst_ref=dst, send_sem=send_sem.at[index], recv_sem=recv_sem.at[index], device_id=device, device_id_type=MESH)
        copy.start()
        started.append(copy)
        return copy

    def load(src, dst):
        copy = pltpu.make_async_copy(src, dst, load_sem.at[len(loads)])
        copy.start()
        loads.append(copy)
        return copy

    def columns_loop(body, init=0, start=0, length=SLAB):
        def step(index, carry):
            return body(pl.ds(pl.multiple_of(start + index * STEP_COLS, 128), STEP_COLS), carry)
        return lax.fori_loop(0, length // STEP_COLS, step, init)

    def add_into(target, terms, start=0, length=SLAB, shift=0):
        def body(cols, carry):
            for tile in range(TILES):
                total = None
                for term in terms:
                    value = term[tile, :, cols].astype(jnp.float32)
                    total = value if total is None else total + value
                target[tile, :, cols] = total
            return carry
        columns_loop(body, 0, start, length)

    peers = [(0, 0, k, 0) for k in (1, 2, 3)] + [(0, k, 0, 0) for k in (1, 2, 3)]
    peers += [(0, 0, k, 1) for k in (1, 3)] + [(0, k, 0, 1) for k in (1, 3)]
    peers += [group for sum_round in SUM_ROUNDS for group in sum_round if group not in peers]
    if (0, 0, 0, 1) not in peers:
        peers.append((0, 0, 0, 1))
    barrier = pltpu.get_barrier_semaphore()
    for offsets in peers:
        pl.semaphore_signal(barrier, inc=1, device_id=peer(*offsets), device_id_type=MESH)

    order = [(1, db) for db in MINUS_SET] + [(3, db) for db in PLUS_SET] + [(1, PLUS_SET[0]), (3, MINUS_SET[0]), (1, PLUS_SET[1]), (3, MINUS_SET[1])]
    order += [(0, db) for db in (2, 3, 0, 1)]
    place = {key: index for index, key in enumerate(order)}
    own_load = {key: load(slab_of(grads, *key), own_raw.at[place[key]]) for key in order}
    state_load = [load(src, dst) for src, dst in ((master_in, master), (one_in, one), (two_in, two))]

    pl.semaphore_wait(barrier, len(peers))

    raw_copy = {}
    for index in range(2):
        for sign, group in ((1, PLUS_SET), (-1, MINUS_SET)):
            for other in (0, 1):
                buffer = relay_raw.at[0 if sign == 1 else 1, other, index]
                raw_copy[sign, other, index] = remote(slab_of(grads, 2, group[index], other), buffer, ring_a(sign, other))
    pair_copy = {key: remote(slab_of(grads, *key, other=1), pair_raw.at[place[key]], peer(0, 0, 0, 1)) for key in order}

    for copy in state_load:
        copy.wait()

    def weight_square(cols, carry):
        return tuple(carry[tile] + master[tile, :, cols] * master[tile, :, cols] for tile in range(TILES))

    def fold(value):
        parts = [value[:, 128 * k:128 * (k + 1)] for k in range(STEP_COLS // 128)]
        while len(parts) > 1:
            parts = [left + right for left, right in zip(parts[::2], parts[1::2])] + parts[len(parts) - len(parts) % 2:]
        return parts[0]

    zero = jnp.zeros((8, STEP_COLS), jnp.float32)
    weight_sq = [jnp.sum(fold(value), axis=1, keepdims=True) for value in columns_loop(weight_square, (zero,) * TILES)]

    def pair_terms(key):
        own_load[key].wait()
        pair_copy[key].wait_recv()
        return [own_raw.at[place[key]], pair_raw.at[place[key]]]

    fin_copy = {}
    for index in range(2):
        for sign, da, group in ((1, 1, MINUS_SET), (-1, 3, PLUS_SET)):
            db, side = group[index], 0 if sign == 1 else 1
            add_into(early.at[side, index], pair_terms((da, db)))
            fin_copy[sign, db] = remote(early.at[side, index], fin.at[side, db], ring_a(sign))
    for index in range(2):
        for sign, da, group in ((1, 1, PLUS_SET), (-1, 3, MINUS_SET)):
            db, side = group[index], 0 if sign == 1 else 1
            terms = pair_terms((da, db))
            for other in (0, 1):
                raw_copy[sign, other, index].wait_recv()
                terms.append(relay_raw.at[side, other, index])
            add_into(late.at[side, index], terms)
            fin_copy[sign, db] = remote(late.at[side, index], fin.at[side, db], ring_a(sign))

    def first_sum(db):
        terms = pair_terms((0, db))
        for sign in (1, -1):
            fin_copy[sign, db].wait_recv()
            terms.append(fin.at[0 if sign == 1 else 1, db])
        add_into(sums.at[db], terms)

    def half(ref, index):
        return ref.at[:, :, pl.ds(index * HALF, HALF)]

    first_sum(2)
    mid_plus = remote(half(sums.at[2], 0), mid.at[0], ring_b(1))
    mid_minus = remote(half(sums.at[2], 1), mid.at[1], ring_b(-1))
    first_sum(3)
    end_minus = [remote(half(sums.at[3], 0), half(end.at[1], 0), ring_b(-1))]
    first_sum(1)
    end_plus = [remote(half(sums.at[1], 1), half(end.at[0], 1), ring_b(1))]

    def add_half(target, extra, half_index):
        def body(index, carry):
            cols = pl.ds(pl.multiple_of(index * STEP_COLS, 128), STEP_COLS)
            wide = pl.ds(pl.multiple_of(half_index * HALF + index * STEP_COLS, 128), STEP_COLS)
            for tile in range(TILES):
                target[tile, :, wide] = target[tile, :, wide] + extra[tile, :, cols]
            return carry
        lax.fori_loop(0, HALF // STEP_COLS, body, 0)

    mid_plus.wait_recv()
    add_half(sums.at[1], mid.at[0], 0)
    end_plus.append(remote(half(sums.at[1], 0), half(end.at[0], 0), ring_b(1)))
    mid_minus.wait_recv()
    add_half(sums.at[3], mid.at[1], 1)
    end_minus.append(remote(half(sums.at[3], 1), half(end.at[1], 1), ring_b(-1)))
    first_sum(0)
    for copy in end_plus + end_minus:
        copy.wait_recv()

    def gather_sum(cols, carry):
        for tile in range(TILES):
            total = sums[0, tile, :, cols] + end[0, tile, :, cols] + end[1, tile, :, cols]
            grad_sum[tile, :, cols] = total
            carry = carry + total * total
        return carry

    def global_sum(first, value):
        for index, group in enumerate(SUM_ROUNDS):
            tiles[first + index] = value
            copies = [remote(tiles.at[first + index], slots.at[first + index, slot], peer(*offsets)) for slot, offsets in enumerate(group)]
            for copy in copies:
                copy.wait_recv()
            for slot in range(len(group)):
                value = value + slots[first + index, slot]
        return value

    grad_sq = global_sum(0, fold(columns_loop(gather_sum, zero)))
    norm_sq = jnp.sum(jnp.sum(grad_sq, axis=0, keepdims=True), axis=1, keepdims=True) / (REPLICAS * REPLICAS)
    clip = jnp.minimum(1.0, MAX_NORM / jnp.sqrt(norm_sq)) / REPLICAS

    def moments(cols, carry):
        squares = []
        for tile in range(TILES):
            scaled = clip * grad_sum[tile, :, cols]
            new_one = BETA_ONE * one[tile, :, cols] + (1.0 - BETA_ONE) * scaled
            new_two = BETA_TWO * two[tile, :, cols] + (1.0 - BETA_TWO) * scaled * scaled
            step = (new_one / CORR_ONE) / (jnp.sqrt(new_two / CORR_TWO) + EPSILON) + WEIGHT_DECAY * master[tile, :, cols]
            one_out[tile, :, cols] = new_one
            two_out[tile, :, cols] = new_two
            direction[tile, :, cols] = step
            squares.append(carry[tile] + step * step)
        return tuple(squares)

    step_sq = [jnp.sum(fold(value), axis=1, keepdims=True) for value in columns_loop(moments, (zero,) * TILES)]

    lane = lax.broadcasted_iota(jnp.int32, (8, 128), 1)
    sub = lax.broadcasted_iota(jnp.int32, (8, 128), 0)
    row_sums = jnp.zeros((8, 128), jnp.float32)
    for index, value in enumerate(step_sq + weight_sq):
        row_sums = jnp.where(lane == index, value, row_sums)

    def tensor_of(sublane):
        row = 8 * jnp.where(lane >= 3, lane - 3, lane) + sublane
        layer = jnp.where(row >= 12, 1, 0)
        block = row - 12 * layer
        return 4 * layer + jnp.where(block >= 3, 1, 0) + jnp.where(block >= 4, 1, 0) + jnp.where(block >= 8, 1, 0)

    row_sums = global_sum(len(SUM_ROUNDS), row_sums)
    tensor_sums = row_sums
    for shift in range(1, 8):
        moved = jnp.where(sub >= shift, sub - shift, sub - shift + 8)
        tensor_sums = tensor_sums + jnp.where(tensor_of(moved) == tensor_of(sub), pltpu.roll(row_sums, shift, 0), 0.0)
    norms = jnp.sqrt(tensor_sums)
    ratio = pltpu.roll(norms, 125, 1) / norms
    rate = [LEARN_RATE * jnp.sum(jnp.where(lane == tile, ratio, 0.0), axis=1, keepdims=True) for tile in range(TILES)]

    own_column = column(0, 0)

    def weights(index, carry):
        cols = pl.ds(pl.multiple_of(index * STEP_COLS, 128), STEP_COLS)
        wide = pl.ds(pl.multiple_of(own_column + index * STEP_COLS, 128), STEP_COLS)
        for tile in range(TILES):
            value = master[tile, :, cols] - rate[tile] * direction[tile, :, cols]
            master_out[tile, :, cols] = value
            params[tile, :, wide] = value.astype(jnp.bfloat16)
        return carry

    lax.fori_loop(0, SLAB // STEP_COLS, weights, 0)

    handed = []

    def spread(ref):
        return remote(ref, ref, ring_a(1)), remote(ref, ref, ring_a(-1))

    def hand(ref):
        handed.append(remote(ref, ref, peer(0, 0, 0, 1)))

    mine = slab_of(params, 0, 0)
    ring_copy = remote(mine, mine, ring_b(1)), remote(mine, mine, ring_b(-1))
    spread_copy = {0: spread(mine)}
    hand(mine)
    far = []
    for side, db in ((0, 3), (1, 1)):
        ring_copy[side].wait_recv()
        far.append(remote(half_of(params, 0, db, side), half_of(params, 0, db, side), ring_b(1 if side == 0 else -1)))
        spread_copy[db] = spread(slab_of(params, 0, db))
        hand(slab_of(params, 0, db))

    def relay(db):
        for side, da in ((0, 3), (1, 1)):
            spread_copy[db][side].wait_recv()
            ref = half_of(params, da, db, side)
            relayed.append((da, db, side, remote(ref, ref, ring_a(1 if side == 0 else -1))))
            hand(slab_of(params, da, db))

    relayed = []
    relay(0)
    far_spread = []
    for side in (0, 1):
        far[side].wait_recv()
        far_spread.append(spread(half_of(params, 0, 2, side)))
        hand(half_of(params, 0, 2, side))
    relay(3)
    relay(1)
    for half_index in (0, 1):
        for side, da in ((0, 3), (1, 1)):
            far_spread[half_index][side].wait_recv()
            ref = half_of(params, da, 2, half_index)
            if side == half_index:
                relayed.append((da, 2, side, remote(ref, ref, ring_a(1 if side == 0 else -1))))
            hand(ref)
    for da, db, side, copy in relayed:
        copy.wait_recv()
        hand(half_of(params, 2, db, side))
    for copy in handed:
        copy.wait_recv()
    for copy in started:
        copy.wait_send()


def solution(mesh):
    state_spec = P(None, ('model', 'data'))

    def device_step(local_grads, master, moment_one, moment_two):
        state = (TILES, 8, SLAB)
        width = local_grads.shape[2]
        hbm = pl.BlockSpec(memory_space=pltpu.HBM)
        vmem = pl.BlockSpec(memory_space=pltpu.VMEM)

        def slabs(count, dtype, length=SLAB):
            return pltpu.VMEM(count + (TILES, 8, length), dtype)

        outs = pl.pallas_call(
            lamb_kernel,
            name='lamb_step',
            out_shape=(
                jax.ShapeDtypeStruct((TILES, 8, width), jnp.bfloat16),
                jax.ShapeDtypeStruct(state, jnp.float32),
                jax.ShapeDtypeStruct(state, jnp.float32),
                jax.ShapeDtypeStruct(state, jnp.float32),
            ),
            in_specs=[hbm] * 4,
            out_specs=(vmem,) * 4,
            scratch_shapes=[
                slabs((12,), jnp.bfloat16),
                slabs((12,), jnp.bfloat16),
                slabs((2, 2, 2), jnp.bfloat16),
                slabs((2, 2), jnp.float32),
                slabs((2, 2), jnp.float32),
                slabs((2, 4), jnp.float32),
                slabs((4,), jnp.float32),
                slabs((2,), jnp.float32, HALF),
                slabs((2,), jnp.float32),
                slabs((), jnp.float32),
                slabs((), jnp.float32),
                slabs((), jnp.float32),
                slabs((), jnp.float32),
                slabs((), jnp.float32),
                pltpu.VMEM((2 * len(SUM_ROUNDS), 8, 128), jnp.float32),
                pltpu.VMEM((2 * len(SUM_ROUNDS), SLOTS, 8, 128), jnp.float32),
                pltpu.SemaphoreType.DMA((COPIES,)),
                pltpu.SemaphoreType.DMA((COPIES,)),
                pltpu.SemaphoreType.DMA((LOADS,)),
            ],
            compiler_params=pltpu.CompilerParams(collective_id=0, has_side_effects=True),
        )(
            local_grads.reshape(TILES, 8, width),
            master.reshape(state),
            moment_one.reshape(state),
            moment_two.reshape(state),
        )
        return tuple(out.reshape(24, -1) for out in outs)

    return jax.shard_map(device_step, mesh=mesh, in_specs=(P('data', None, 'model'), state_spec, state_spec, state_spec), out_specs=(P(None, 'model'), state_spec, state_spec, state_spec), check_vma=False)
```

time: 309 us -> 110 us (0.36)
  blocking collectives: 225 us -> 0 us
  Pallas kernels: 0 us -> 100 us
  waiting for transfers between devices: 48 us -> 0 us
  between operations: 14.8 us -> 0.67 us
  local copies, waits for them, and re-layouts: 16.9 us -> 9.29 us
  other arithmetic: 4.01 us -> 0 us
    psum x2 -> x0, blocking collectives: 128 us -> none  [the longest x1 65.9 us: device_step(): total_sq = lax.psum(jnp.sum(grad_mean * grad_mean), both_axes)]
    pallas_call x0 -> x1, Pallas kernels: none -> 100 us  [device_step(): pl.pallas_call(lamb_kernel, name='lamb_step', out_shape=(jax.ShapeDtypeSt...]
    all_to_all x1 -> x0, blocking collectives: 96.6 us -> none  [device_step(): received = lax.all_to_all(grad_slab, 'data', 1, 0, tiled=True)]
    all_gather x1 -> x0, waiting for transfers between devices: 47.9 us -> none  [device_step(): lax.all_gather(new_master.astype(jnp.bfloat16), 'data', axis=1, tiled=True)]
    all_to_all x1 -> x0, local copies, waits for them, and re-layouts: 3.88 us -> none  [device_step(): received = lax.all_to_all(grad_slab, 'data', 1, 0, tiled=True)]
    unnamed x12 -> x10, local copies, waits for them, and re-layouts: 12.1 us -> 9.29 us
  transfers between devices with their start and end apart: 1 -> 0, of which waited for: 1 -> 0; matrix products, arithmetic and copies ran while one was open for 0% -> 0% of each run, Pallas kernels for 0% -> 0%
where the time goes in v1:
time: 110 us
  Pallas kernels  100 us (91%)
  local copies, waits for them, and re-layouts  9.29 us (8%)
    pallas_call x1, Pallas kernels, device_step(): pl.pallas_call(lamb_kernel, name='lamb_step', out_shape=(jax.ShapeDtypeSt...  100 us
    unnamed x10, local copies, waits for them, and re-layouts  9.29 us

profile of v1, /device:TPU:1, one launch (start us, length us, event | category | flops | bytes accessed | tf_op | source)
XLA Modules:
  0.0 110.3 jit_solution(4956219109110910885)
XLA Ops:
  0.6 100.4 %lamb_step.1 = (bf16[3,8,147456]{2,1,0:T(8,128)(2,1)}, f32[3,8,4608]{2,1,0:T(8,128)}, f32[3,8,4608]{2,1,0:T(8,128)}, f32[3,8,4608]{2,1,0:T(8,128)}) custom-call(bf16[3,8,147456]{2,1,0:T(8,128)(2,1)} %bitcast.9, f32[3,8,4608]{2,1,0:T(8,128)} %bitcast.13, f32[3,8,4608]{2,1,0:T(8,128)} %bitcast.14, f32[3,8,4608]{2,1,0:T(8,128)} %bitcast.15), custom_call_target="tpu_custom_call" | custom-call | tf_op jit(solution)/shard_map/lamb_step/pallas_call | solution.py:327
  101.0 0.0 copy-start.2
  101.0 0.0 copy-start.1
  101.0 0.0 copy-start
  101.0 7.0 %copy.12 = bf16[24,147456]{1,0:T(8,128)(2,1)} copy(bf16[24,147456]{1,0:T(8,128)(2,1)} %bitcast.8) | data formatting | bytes 14155776
  108.0 0.0 copy-done.2
  108.0 0.8 copy.13
  108.8 0.0 copy-done.1
  108.8 0.8 copy.14
  109.6 0.0 copy-done
  109.6 0.8 copy.15
Async XLA Ops:
  101.0 7.0 %copy-start.2 = (f32[3,8,4608]{2,1,0:T(8,128)S(1)}, f32[3,8,4608]{2,1,0:T(8,128)}, u32[]{:S(2)}) copy-start(f32[3,8,4608]{2,1,0:T(8,128)} %get-tuple-element.9) | copy-start | bytes 1327108
  101.0 7.8 %copy-start.1 = (f32[3,8,4608]{2,1,0:T(8,128)S(1)}, f32[3,8,4608]{2,1,0:T(8,128)}, u32[]{:S(2)}) copy-start(f32[3,8,4608]{2,1,0:T(8,128)} %get-tuple-element.10) | copy-start | bytes 1327108
  101.0 8.5 %copy-start = (f32[3,8,4608]{2,1,0:T(8,128)S(1)}, f32[3,8,4608]{2,1,0:T(8,128)}, u32[]{:S(2)}) copy-start(f32[3,8,4608]{2,1,0:T(8,128)} %get-tuple-element.11) | copy-start | bytes 1327108

commit v2 on v1

--- a/solution.py
+++ b/solution.py
@@ -33,6 +33,7 @@
 SLOTS = max(len(group) for group in SUM_ROUNDS)
 COPIES = 120
 LOADS = 18
+VMEM_LIMIT = 40 * 2 ** 20
 
 
 def lamb_kernel(grads, master_in, one_in, two_in, params, master_out, one_out, two_out, own_raw, pair_raw, relay_raw, early, late, fin, sums, mid, end, master, one, two, grad_sum, direction, tiles, slots, send_sem, recv_sem, load_sem):
@@ -324,14 +325,15 @@
         def slabs(count, dtype, length=SLAB):
             return pltpu.VMEM(count + (TILES, 8, length), dtype)
 
+        operands = (local_grads.reshape(TILES, 8, width), master.reshape(state), moment_one.reshape(state), moment_two.reshape(state))
         outs = pl.pallas_call(
             lamb_kernel,
             name='lamb_step',
             out_shape=(
-                jax.ShapeDtypeStruct((TILES, 8, width), jnp.bfloat16),
-                jax.ShapeDtypeStruct(state, jnp.float32),
-                jax.ShapeDtypeStruct(state, jnp.float32),
-                jax.ShapeDtypeStruct(state, jnp.float32),
+                pltpu.VMEM((TILES, 8, width), jnp.bfloat16),
+                pltpu.VMEM(state, jnp.float32),
+                pltpu.VMEM(state, jnp.float32),
+                pltpu.VMEM(state, jnp.float32),
             ),
             in_specs=[hbm] * 4,
             out_specs=(vmem,) * 4,
@@ -356,12 +358,9 @@
                 pltpu.SemaphoreType.DMA((COPIES,)),
                 pltpu.SemaphoreType.DMA((LOADS,)),
             ],
-            compiler_params=pltpu.CompilerParams(collective_id=0, has_side_effects=True),
+            compiler_params=pltpu.CompilerParams(collective_id=0, has_side_effects=True, vmem_limit_bytes=VMEM_LIMIT),
         )(
-            local_grads.reshape(TILES, 8, width),
-            master.reshape(state),
-            moment_one.reshape(state),
-            moment_two.reshape(state),
+            *(pltpu.with_memory_space_constraint(operand, pltpu.HBM) for operand in operands)
         )
         return tuple(out.reshape(24, -1) for out in outs)
 

time: 110 us -> 103 us (0.936)
  local copies, waits for them, and re-layouts: 9.29 us -> 5.25 us
  Pallas kernels: 100 us -> 97.1 us
    unnamed x10 -> x4, local copies, waits for them, and re-layouts: 9.29 us -> 5.25 us
    pallas_call x1, Pallas kernels: 100 us -> 97.1 us  [device_step(): pl.pallas_call(lamb_kernel, name='lamb_step', out_shape=(pltpu.VMEM((TILE...]
where the time goes in v2:
time: 103 us
  Pallas kernels  97.1 us (94%)
  local copies, waits for them, and re-layouts  5.25 us (5%)
    pallas_call x1, Pallas kernels, device_step(): pl.pallas_call(lamb_kernel, name='lamb_step', out_shape=(pltpu.VMEM((TILE...  97.1 us
    unnamed x4, local copies, waits for them, and re-layouts  5.25 us

profile of v2, /device:TPU:1, one launch (start us, length us, event | category | flops | bytes accessed | tf_op | source)
XLA Modules:
  0.0 103.0 jit_solution(14042166001458126830)
XLA Ops:
  0.6 97.1 %lamb_step.1 = (bf16[3,8,147456]{2,1,0:T(8,128)(2,1)S(1)}, f32[3,8,4608]{2,1,0:T(8,128)S(1)}, f32[3,8,4608]{2,1,0:T(8,128)S(1)}, f32[3,8,4608]{2,1,0:T(8,128)S(1)}) custom-call(bf16[3,8,147456]{2,1,0:T(8,128)(2,1)} %bitcast.12, f32[3,8,4608]{2,1,0:T(8,128)} %bitcast.13, f32[3,8,4608]{2,1,0:T(8,128)} %bitcast.14, f32[3,8,4608]{2,1,0:T(8,128)} %bitcast.15), custom_call_target="tpu_custom_call" | custom-call | tf_op jit(solution)/shard_map/lamb_step/pallas_call | solution.py:329
  97.7 3.0 %copy.12 = bf16[24,147456]{1,0:T(8,128)(2,1)} copy(bf16[24,147456]{1,0:T(8,128)(2,1)S(1)} %bitcast.8) | data formatting | bytes 14155776
  100.7 0.8 copy.13
  101.5 0.8 copy.14
  102.2 0.8 copy.15

commit v3 on v0

v3 whole, which is shorter than its diff:
```python
import functools

import jax
import jax.numpy as jnp
from jax import lax
from jax.experimental import pallas as pl
from jax.experimental.pallas import tpu as pltpu
from jax.sharding import PartitionSpec as P

STEP = 4
LEARN_RATE = 0.08
BETA_ONE = 0.9
BETA_TWO = 0.999
EPSILON = 1e-6
WEIGHT_DECAY = 0.01
MAX_NORM = 1.0
CORR_ONE = 1.0 - BETA_ONE ** STEP
CORR_TWO = 1.0 - BETA_TWO ** STEP

MESH = pl.DeviceIdType.MESH
TILES = 3
SLAB = 4608
HALF = SLAB // 2
STEP_COLS = 768
REPLICAS = 32
LATE = (((2, 0), (1, 1), (1, 0), (0, 0)), ((2, 1), (3, 0), (3, 1), (0, 1)))
EARLY = (((3, 0), (3, 1), (2, 1), (0, 1)), ((1, 1), (1, 0), (2, 0), (0, 0)))
PIECES = 4
ORDER = ((1, 3), (3, 1), (1, 2), (3, 2), (1, 0), (3, 0), (1, 1), (3, 3), (0, 2), (0, 1), (0, 3), (0, 0))
PLANE = tuple((0, k, e, 0) for k in range(4) for e in range(4) if (k, e) != (0, 0))
ACROSS = tuple((k, 0, 0, e) for k in range(4) for e in range(2) if (k, e) != (0, 0))
SUM_ROUNDS = (PLANE, ACROSS)
SLOTS = len(PLANE)
BARRIER = ACROSS + tuple((0, k, 0, e) for k in (1, 3) for e in (0, 1)) + tuple((0, 0, k, e) for k in (1, 3) for e in (0, 1))
COPIES = 180
LOADS = len(ORDER) + 3
VMEM_LIMIT = 40 * 2 ** 20
WRITE_PIECES = 4


def lamb_kernel(grads, master_in, one_in, two_in, params, master_out, one_out, two_out, own_raw, pair_raw, relay_raw, early, late, fin, sums, mid, end, master, one, two, grad_sum, direction, rows, slots, send_sem, recv_sem, load_sem):
    x, data = lax.axis_index('model'), lax.axis_index('data')
    core, y, z = lax.rem(data, 2), lax.rem(data // 2, 4), data // 8
    started = []
    loads = []

    def peer(dx, dz, dy, dc):
        chip = lax.rem(z + dz + 4, 4) * 4 + lax.rem(y + dy + 4, 4)
        return lax.rem(x + dx, 4), chip * 2 + lax.rem(core + dc, 2)

    def ring_a(side, other=0):
        role = core if not other else 1 - core
        step = 1 - 2 * side
        return peer(0, step * role, step * (1 - role), other)

    def ring_b(side):
        step = 1 - 2 * side
        return peer(0, step * (1 - core), step * core, 0)

    partner = peer(0, 0, 0, 1)

    def column(da, db, other=0):
        role = core if not other else 1 - core
        dy, dz = da * (1 - role) + db * role, da * role + db * (1 - role)
        slab = (lax.rem(z + dz, 4) * 4 + lax.rem(y + dy, 4)) * 2 + role
        return pl.multiple_of(slab * SLAB, SLAB)

    def whole(ref, da, db, other=0):
        return ref.at[:, :, pl.ds(column(da, db, other), SLAB)]

    def piece(ref, da, db, half, other=0):
        return ref.at[:, :, pl.ds(pl.multiple_of(column(da, db, other) + half * HALF, HALF), HALF)]

    def part(ref, half):
        return ref.at[:, :, pl.ds(half * HALF, HALF)]

    def remote(src, dst, device):
        index = len(started)
        copy = pltpu.make_async_remote_copy(src_ref=src, dst_ref=dst, send_sem=send_sem.at[index], recv_sem=recv_sem.at[index], device_id=device, device_id_type=MESH)
        copy.start()
        started.append(copy)
        return copy

    def load(src, dst):
        copy = pltpu.make_async_copy(src, dst, load_sem.at[len(loads)])
        copy.start()
        loads.append(copy)
        return copy

    def columns_loop(body, init=0, length=SLAB):
        def step(index, carry):
            return body(index * STEP_COLS, carry)
        return lax.fori_loop(0, length // STEP_COLS, step, init)

    def at(start):
        return pl.ds(pl.multiple_of(start, 128), STEP_COLS)

    def add_half(target, target_start, terms):
        def body(offset, carry):
            for tile in range(TILES):
                total = None
                for term, start in terms:
                    value = term[tile, :, at(start + offset)].astype(jnp.float32)
                    total = value if total is None else total + value
                target[tile, :, at(target_start + offset)] = total
            return carry
        columns_loop(body, 0, HALF)

    barrier = pltpu.get_barrier_semaphore()
    for offsets in BARRIER:
        pl.semaphore_signal(barrier, inc=1, device_id=peer(*offsets), device_id_type=MESH)

    place = {key: index for index, key in enumerate(ORDER)}
    own_load = {key: load(whole(grads, *key), own_raw.at[place[key]]) for key in ORDER}
    state_load = [load(src, dst) for src, dst in ((master_in, master), (one_in, one), (two_in, two))]

    pl.semaphore_wait(barrier, len(BARRIER))

    raw_copy = {}
    for index in range(PIECES):
        for side in (0, 1):
            for other in (0, 1):
                db, half = LATE[side][index]
                raw_copy[side, other, index] = remote(piece(grads, 2, db, half, other), relay_raw.at[side, other, index], ring_a(side, other))
    pair_copy = {key: remote(whole(grads, *key, other=1), pair_raw.at[place[key]], partner) for key in ORDER}

    def fold(value):
        parts = [value[:, 128 * k:128 * (k + 1)] for k in range(STEP_COLS // 128)]
        while len(parts) > 1:
            parts = [left + right for left, right in zip(parts[::2], parts[1::2])] + parts[len(parts) - len(parts) % 2:]
        return parts[0]

    def weight_square(offset, carry):
        return tuple(carry[tile] + master[tile, :, at(offset)] * master[tile, :, at(offset)] for tile in range(TILES))

    for copy in state_load:
        copy.wait()
    zero = jnp.zeros((8, STEP_COLS), jnp.float32)
    weight_sq = [jnp.sum(fold(value), axis=1, keepdims=True) for value in columns_loop(weight_square, (zero,) * TILES)]

    ready = set()

    def pair_terms(da, db, half):
        key = (da, db)
        if key not in ready:
            own_load[key].wait()
            pair_copy[key].wait_recv()
            ready.add(key)
        return [(own_raw.at[place[key]], half * HALF), (pair_raw.at[place[key]], half * HALF)]

    fin_copy = {}
    for index in range(PIECES):
        for side in (0, 1):
            db, half = EARLY[side][index]
            add_half(early.at[side, index], 0, pair_terms(1 + 2 * side, db, half))
            fin_copy[side, db, half] = remote(early.at[side, index], part(fin.at[side, db], half), ring_a(side))
    for index in range(PIECES):
        for side in (0, 1):
            db, half = LATE[side][index]
            terms = pair_terms(1 + 2 * side, db, half)
            for other in (0, 1):
                raw_copy[side, other, index].wait_recv()
                terms.append((relay_raw.at[side, other, index], 0))
            add_half(late.at[side, index], 0, terms)
            fin_copy[side, db, half] = remote(late.at[side, index], part(fin.at[side, db], half), ring_a(side))

    def first_sum(db, half):
        terms = pair_terms(0, db, half)
        for side in (0, 1):
            fin_copy[side, db, half].wait_recv()
            terms.append((fin.at[side, db], half * HALF))
        add_half(sums.at[db], half * HALF, terms)

    mid_copy = {}
    end_copy = {}
    for side in (0, 1):
        first_sum(2, side)
        mid_copy[side] = remote(part(sums.at[2], side), mid.at[side], ring_b(side))
    for side in (0, 1):
        db, half = 1 + 2 * side, 1 - side
        first_sum(db, half)
        end_copy[side, half] = remote(part(sums.at[db], half), part(end.at[side], half), ring_b(side))
    for side in (0, 1):
        first_sum(1 + 2 * side, side)
    for side in (0, 1):
        db = 1 + 2 * side
        mid_copy[side].wait_recv()
        add_half(sums.at[db], side * HALF, [(sums.at[db], side * HALF), (mid.at[side], 0)])
        end_copy[side, side] = remote(part(sums.at[db], side), part(end.at[side], side), ring_b(side))
    for side in (0, 1):
        first_sum(0, side)
    for side in (0, 1):
        end_copy[side, 1 - side].wait_recv()
    for side in (0, 1):
        end_copy[side, side].wait_recv()

    def gather_sum(offset, carry):
        for tile in range(TILES):
            total = sums[0, tile, :, at(offset)] + end[0, tile, :, at(offset)] + end[1, tile, :, at(offset)]
            grad_sum[tile, :, at(offset)] = total
            carry = carry + total * total
        return carry

    def global_sum(first, value):
        for index, group in enumerate(SUM_ROUNDS):
            rows[first + index] = value
            copies = [remote(rows.at[first + index], slots.at[first + index, slot], peer(*offsets)) for slot, offsets in enumerate(group)]
            for copy in copies:
                copy.wait_recv()
            received = [slots[first + index, slot] for slot in range(len(group))] + [value]
            while len(received) > 1:
                received = [left + right for left, right in zip(received[::2], received[1::2])]
            value = received[0]
        return value

    grad_sq = global_sum(0, jnp.sum(fold(columns_loop(gather_sum, zero)), axis=0, keepdims=True))
    norm_sq = jnp.sum(grad_sq, axis=1, keepdims=True) / (REPLICAS * REPLICAS)
    clip = jnp.minimum(1.0, MAX_NORM / jnp.sqrt(norm_sq)) / REPLICAS

    def moments(offset, carry):
        squares = []
        for tile in range(TILES):
            scaled = clip * grad_sum[tile, :, at(offset)]
            new_one = BETA_ONE * one[tile, :, at(offset)] + (1.0 - BETA_ONE) * scaled
            new_two = BETA_TWO * two[tile, :, at(offset)] + (1.0 - BETA_TWO) * scaled * scaled
            step = (new_one * (1.0 / CORR_ONE)) / (jnp.sqrt(new_two * (1.0 / CORR_TWO)) + EPSILON) + WEIGHT_DECAY * master[tile, :, at(offset)]
            one_out[tile, :, at(offset)] = new_one
            two_out[tile, :, at(offset)] = new_two
            direction[tile, :, at(offset)] = step
            squares.append(carry[tile] + step * step)
        return tuple(squares)

    step_sq = [jnp.sum(fold(value), axis=1, keepdims=True) for value in columns_loop(moments, (zero,) * TILES)]

    lane = lax.broadcasted_iota(jnp.int32, (8, 128), 1)
    sub = lax.broadcasted_iota(jnp.int32, (8, 128), 0)
    spread_sums = jnp.zeros((8, 128), jnp.float32)
    for tile in range(TILES):
        spread_sums = jnp.where(lane == 8 * tile + sub, step_sq[tile], spread_sums)
        spread_sums = jnp.where(lane == 32 + 8 * tile + sub, weight_sq[tile], spread_sums)

    def tensor_of(row):
        layer = jnp.where(row >= 12, 1, 0)
        block = row - 12 * layer
        return 4 * layer + jnp.where(block >= 3, 1, 0) + jnp.where(block >= 4, 1, 0) + jnp.where(block >= 8, 1, 0)

    row_sums = jnp.broadcast_to(global_sum(len(SUM_ROUNDS), jnp.sum(spread_sums, axis=0, keepdims=True)), (8, 128))
    rate = []
    for tile in range(TILES):
        tensor = tensor_of(8 * tile + sub)
        step_mask = (tensor_of(lane) == tensor) & (lane < 24)
        weight_mask = (tensor_of(lane - 32) == tensor) & (lane >= 32) & (lane < 56)
        step_norm = jnp.sqrt(jnp.sum(jnp.where(step_mask, row_sums, 0.0), axis=1, keepdims=True))
        weight_norm = jnp.sqrt(jnp.sum(jnp.where(weight_mask, row_sums, 0.0), axis=1, keepdims=True))
        rate.append(LEARN_RATE * (weight_norm / step_norm))

    own_column = column(0, 0)

    def weights(offset, carry):
        for tile in range(TILES):
            value = master[tile, :, at(offset)] - rate[tile] * direction[tile, :, at(offset)]
            master_out[tile, :, at(offset)] = value
            params[tile, :, at(own_column + offset)] = value.astype(jnp.bfloat16)
        return carry

    columns_loop(weights)

    handed = []
    along_b = {}
    along_a = {}
    far_b = {}
    far_a = {}

    def send(da, db, half, device):
        ref = piece(params, da, db, half)
        return remote(ref, ref, device)

    def hand(da, db, half):
        handed.append(send(da, db, half, partner))

    def pass_on(first, second):
        for one_piece, other_piece in ((first, second), (second, first)):
            along_a[0, one_piece] = send(0, *one_piece, ring_a(0))
            along_a[1, other_piece] = send(0, *other_piece, ring_a(1))

    for order in (0, 1):
        for side in (0, 1):
            half = side if order == 0 else 1 - side
            along_b[side, half] = send(0, 0, half, ring_b(side))
        for side in (0, 1):
            half = side if order == 0 else 1 - side
            along_a[side, (0, half)] = send(0, 0, half, ring_a(side))
    hand(0, 0, 0)
    hand(0, 0, 1)

    def arrived(side, db, half):
        along_a[side, (db, half)].wait_recv()
        da = 3 - 2 * side
        if half == side:
            far_a[db, half] = send(da, db, half, ring_a(side))
        hand(da, db, half)

    for side in (0, 1):
        db = 3 - 2 * side
        along_b[side, side].wait_recv()
        far_b[side] = send(0, db, side, ring_b(side))
    pass_on((3, 0), (1, 1))
    hand(0, 3, 0)
    hand(0, 1, 1)
    for side in (0, 1):
        arrived(side, 0, side)
    for side in (0, 1):
        along_b[side, 1 - side].wait_recv()
    pass_on((1, 0), (3, 1))
    hand(0, 3, 1)
    hand(0, 1, 0)
    for side in (0, 1):
        arrived(side, 0, 1 - side)
    for side in (0, 1):
        far_b[side].wait_recv()
    pass_on((2, 0), (2, 1))
    hand(0, 2, 0)
    hand(0, 2, 1)
    for pieces in (((3, 0), (1, 1)), ((1, 1), (3, 0)), ((1, 0), (3, 1)), ((3, 1), (1, 0)), ((2, 0), (2, 1)), ((2, 1), (2, 0))):
        for side in (0, 1):
            arrived(side, *pieces[side])
    for db in (0, 3, 1, 2):
        for half in (0, 1):
            far_a[db, half].wait_recv()
            hand(2, db, half)
    for copy in handed:
        copy.wait_recv()
    for copy in started:
        copy.wait_send()


def write_kernel(params, master, one, two, params_out, master_out, one_out, two_out, sem):
    pairs = [(master, master_out), (one, one_out), (two, two_out)]
    width = params.shape[2] // WRITE_PIECES
    for tile in range(TILES):
        for index in range(WRITE_PIECES):
            cols = pl.ds(index * width, width)
            pairs.append((params.at[tile, :, cols], params_out.at[tile, :, cols]))
    copies = [pltpu.make_async_copy(src, dst, sem.at[index]) for index, (src, dst) in enumerate(pairs)]
    for copy in copies:
        copy.start()
    for copy in copies:
        copy.wait()


def solution(mesh):
    state_spec = P(None, ('model', 'data'))

    def device_step(local_grads, master, moment_one, moment_two):
        state = (TILES, 8, SLAB)
        width = local_grads.shape[2]
        hbm = pl.BlockSpec(memory_space=pltpu.HBM)
        vmem = pl.BlockSpec(memory_space=pltpu.VMEM)

        def slabs(count, dtype, length=SLAB):
            return pltpu.VMEM(count + (TILES, 8, length), dtype)

        operands = (local_grads.reshape(TILES, 8, width), master.reshape(state), moment_one.reshape(state), moment_two.reshape(state))
        results = pl.pallas_call(
            lamb_kernel,
            name='lamb_step',
            out_shape=(
                pltpu.VMEM((TILES, 8, width), jnp.bfloat16),
                pltpu.VMEM(state, jnp.float32),
                pltpu.VMEM(state, jnp.float32),
                pltpu.VMEM(state, jnp.float32),
            ),
            in_specs=[hbm] * 4,
            out_specs=(vmem,) * 4,
            scratch_shapes=[
                slabs((len(ORDER),), jnp.bfloat16),
                slabs((len(ORDER),), jnp.bfloat16),
                slabs((2, 2, PIECES), jnp.bfloat16, HALF),
                slabs((2, PIECES), jnp.float32, HALF),
                slabs((2, PIECES), jnp.float32, HALF),
                slabs((2, 4), jnp.float32),
                slabs((4,), jnp.float32),
                slabs((2,), jnp.float32, HALF),
                slabs((2,), jnp.float32),
                slabs((), jnp.float32),
                slabs((), jnp.float32),
                slabs((), jnp.float32),
                slabs((), jnp.float32),
                slabs((), jnp.float32),
                pltpu.VMEM((2 * len(SUM_ROUNDS), 1, 128), jnp.float32),
                pltpu.VMEM((2 * len(SUM_ROUNDS), SLOTS, 1, 128), jnp.float32),
                pltpu.SemaphoreType.DMA((COPIES,)),
                pltpu.SemaphoreType.DMA((COPIES,)),
                pltpu.SemaphoreType.DMA((LOADS,)),
            ],
            compiler_params=pltpu.CompilerParams(collective_id=0, has_side_effects=True, vmem_limit_bytes=VMEM_LIMIT),
        )(*(pltpu.with_memory_space_constraint(operand, pltpu.HBM) for operand in operands))
        outs = pl.pallas_call(
            write_kernel,
            name='write_out',
            out_shape=tuple(pltpu.HBM(result.shape, result.dtype) for result in results),
            in_specs=[vmem] * 4,
            out_specs=(hbm,) * 4,
            scratch_shapes=[pltpu.SemaphoreType.DMA((TILES * WRITE_PIECES + 3,))],
            compiler_params=pltpu.CompilerParams(vmem_limit_bytes=2 ** 20),
        )(*results)
        return tuple(out.reshape(24, -1) for out in outs)

    return jax.shard_map(device_step, mesh=mesh, in_specs=(P('data', None, 'model'), state_spec, state_spec, state_spec), out_specs=(P(None, 'model'), state_spec, state_spec, state_spec), check_vma=False)
```

time: 309 us -> 92.3 us (0.30)
  blocking collectives: 225 us -> 0 us
  Pallas kernels: 0 us -> 91.5 us
  waiting for transfers between devices: 48 us -> 0 us
  local copies, waits for them, and re-layouts: 16.9 us -> 0 us
  between operations: 14.8 us -> 0.64 us
  other arithmetic: 4.01 us -> 0 us
    psum x2 -> x0, blocking collectives: 128 us -> none  [the longest x1 65.9 us: device_step(): total_sq = lax.psum(jnp.sum(grad_mean * grad_mean), both_axes)]
    all_to_all x1 -> x0, blocking collectives: 96.6 us -> none  [device_step(): received = lax.all_to_all(grad_slab, 'data', 1, 0, tiled=True)]
    pallas_call x0 -> x2, Pallas kernels: none -> 91.5 us  [the longest x1 88.1 us: device_step(): pl.pallas_call(lamb_kernel, name='lamb_step', out_shape=(pltpu.VMEM((TILE...]
    all_gather x1 -> x0, waiting for transfers between devices: 47.9 us -> none  [device_step(): lax.all_gather(new_master.astype(jnp.bfloat16), 'data', axis=1, tiled=True)]
    unnamed x12 -> x0, local copies, waits for them, and re-layouts: 12.1 us -> none
    all_to_all x1 -> x0, local copies, waits for them, and re-layouts: 3.88 us -> none  [device_step(): received = lax.all_to_all(grad_slab, 'data', 1, 0, tiled=True)]
  transfers between devices with their start and end apart: 1 -> 0, of which waited for: 1 -> 0; matrix products, arithmetic and copies ran while one was open for 0% -> 0% of each run, Pallas kernels for 0% -> 0%
where the time goes in v3:
time: 92.3 us; the launch traced here: 92.2 us
  Pallas kernels  91.5 us (99%)
    pallas_call x1, Pallas kernels, device_step(): pl.pallas_call(lamb_kernel, name='lamb_step', out_shape=(pltpu.VMEM((TILE...  88.1 us
    pallas_call x1, Pallas kernels, device_step(): pl.pallas_call(write_kernel, name='write_out', out_shape=tuple((pltpu.HBM...  3.42 us

profile of v3, /device:TPU:1, one launch (start us, length us, event | category | flops | bytes accessed | tf_op | source)
XLA Modules:
  0.0 92.2 jit_solution(4877414725720612712)
XLA Ops:
  0.6 88.1 %lamb_step.1 = (bf16[3,8,147456]{2,1,0:T(8,128)(2,1)S(1)}, f32[3,8,4608]{2,1,0:T(8,128)S(1)}, f32[3,8,4608]{2,1,0:T(8,128)S(1)}, f32[3,8,4608]{2,1,0:T(8,128)S(1)}) custom-call(bf16[3,8,147456]{2,1,0:T(8,128)(2,1)} %bitcast.8, f32[3,8,4608]{2,1,0:T(8,128)} %bitcast.9, f32[3,8,4608]{2,1,0:T(8,128)} %bitcast.10, f32[3,8,4608]{2,1,0:T(8,128)} %bitcast.11), custom_call_target="tpu_custom_call" | custom-call | tf_op jit(solution)/shard_map/lamb_step/pallas_call | solution.py:364
  88.7 3.4 %write_out.1 = (bf16[3,8,147456]{2,1,0:T(8,128)(2,1)}, f32[3,8,4608]{2,1,0:T(8,128)}, f32[3,8,4608]{2,1,0:T(8,128)}, f32[3,8,4608]{2,1,0:T(8,128)}) custom-call(bf16[3,8,147456]{2,1,0:T(8,128)(2,1)S(1)} %get-tuple-element.12.params, f32[3,8,4608]{2,1,0:T(8,128)S(1)} %get-tuple-element.13.master, f32[3,8,4608]{2,1,0:T(8,128)S(1)} %get-tuple-element.14.one, ...), custom_call_target="tpu_custom_call" | custom-call | tf_op jit(solution)/shard_map/write_out/pallas_call | solution.py:398

commit v4 on v3

--- a/solution.py
+++ b/solution.py
@@ -27,18 +27,21 @@
 EARLY = (((3, 0), (3, 1), (2, 1), (0, 1)), ((1, 1), (1, 0), (2, 0), (0, 0)))
 PIECES = 4
 ORDER = ((1, 3), (3, 1), (1, 2), (3, 2), (1, 0), (3, 0), (1, 1), (3, 3), (0, 2), (0, 1), (0, 3), (0, 0))
-PLANE = tuple((0, k, e, 0) for k in range(4) for e in range(4) if (k, e) != (0, 0))
-ACROSS = tuple((k, 0, 0, e) for k in range(4) for e in range(2) if (k, e) != (0, 0))
-SUM_ROUNDS = (PLANE, ACROSS)
-SLOTS = len(PLANE)
-BARRIER = ACROSS + tuple((0, k, 0, e) for k in (1, 3) for e in (0, 1)) + tuple((0, 0, k, e) for k in (1, 3) for e in (0, 1))
-COPIES = 180
+EVERY = sorted(((i, j, k, e) for i in range(4) for j in range(4) for k in range(4) for e in range(2) if i + j + k + e), key=lambda far: -sum(min(step, 4 - step) for step in far[:3]) - far[3] / 2)
+DEVICES = len(EVERY) + 1
+ALONG_X = tuple((k, 0, 0, 0) for k in (1, 3))
+ALONG_Z = tuple((0, k, 0, 0) for k in (1, 3))
+ALONG_Y = tuple((0, 0, k, 0) for k in (1, 3))
+OTHER_CORE = ((0, 0, 0, 1),)
+BARRIER = ALONG_X + ALONG_Z + ALONG_Y + OTHER_CORE + tuple((0, k, 0, 1) for k in (1, 3)) + tuple((0, 0, k, 1) for k in (1, 3))
+STAGES = (ALONG_X, OTHER_CORE, ALONG_Y, ALONG_Y, ALONG_Z, ALONG_Z)
+COPIES = 120
 LOADS = len(ORDER) + 3
 VMEM_LIMIT = 40 * 2 ** 20
 WRITE_PIECES = 4
 
 
-def lamb_kernel(grads, master_in, one_in, two_in, params, master_out, one_out, two_out, own_raw, pair_raw, relay_raw, early, late, fin, sums, mid, end, master, one, two, grad_sum, direction, rows, slots, send_sem, recv_sem, load_sem):
+def lamb_kernel(grads, master_in, one_in, two_in, params, master_out, one_out, two_out, own_raw, pair_raw, relay_raw, early, late, fin, sums, mid, end, master, one, two, grad_sum, direction, rows, slots, send_sem, recv_sem, load_sem, sum_send, sum_recv, stage_sem):
     x, data = lax.axis_index('model'), lax.axis_index('data')
     core, y, z = lax.rem(data, 2), lax.rem(data // 2, 4), data // 8
     started = []
@@ -110,6 +113,15 @@
     for offsets in BARRIER:
         pl.semaphore_signal(barrier, inc=1, device_id=peer(*offsets), device_id_type=MESH)
 
+    def stage_signal(stage):
+        for offsets in STAGES[stage]:
+            pl.semaphore_signal(stage_sem.at[stage], inc=1, device_id=peer(*offsets), device_id_type=MESH)
+
+    def stage_next(stage):
+        pl.semaphore_wait(stage_sem.at[stage], len(STAGES[stage]))
+        if stage + 1 < len(STAGES):
+            stage_signal(stage + 1)
+
     place = {key: index for index, key in enumerate(ORDER)}
     own_load = {key: load(whole(grads, *key), own_raw.at[place[key]]) for key in ORDER}
     state_load = [load(src, dst) for src, dst in ((master_in, master), (one_in, one), (two_in, two))]
@@ -123,6 +135,8 @@
                 db, half = LATE[side][index]
                 raw_copy[side, other, index] = remote(piece(grads, 2, db, half, other), relay_raw.at[side, other, index], ring_a(side, other))
     pair_copy = {key: remote(whole(grads, *key, other=1), pair_raw.at[place[key]], partner) for key in ORDER}
+
+    stage_signal(0)
 
     def fold(value):
         parts = [value[:, 128 * k:128 * (k + 1)] for k in range(STEP_COLS // 128)]
@@ -154,6 +168,7 @@
             db, half = EARLY[side][index]
             add_half(early.at[side, index], 0, pair_terms(1 + 2 * side, db, half))
             fin_copy[side, db, half] = remote(early.at[side, index], part(fin.at[side, db], half), ring_a(side))
+        stage_next(index)
     for index in range(PIECES):
         for side in (0, 1):
             db, half = LATE[side][index]
@@ -163,6 +178,8 @@
                 terms.append((relay_raw.at[side, other, index], 0))
             add_half(late.at[side, index], 0, terms)
             fin_copy[side, db, half] = remote(late.at[side, index], part(fin.at[side, db], half), ring_a(side))
+        if PIECES + index < len(STAGES):
+            stage_next(PIECES + index)
 
     def first_sum(db, half):
         terms = pair_terms(0, db, half)
@@ -201,17 +218,22 @@
             carry = carry + total * total
         return carry
 
-    def global_sum(first, value):
-        for index, group in enumerate(SUM_ROUNDS):
-            rows[first + index] = value
-            copies = [remote(rows.at[first + index], slots.at[first + index, slot], peer(*offsets)) for slot, offsets in enumerate(group)]
-            for copy in copies:
-                copy.wait_recv()
-            received = [slots[first + index, slot] for slot in range(len(group))] + [value]
-            while len(received) > 1:
-                received = [left + right for left, right in zip(received[::2], received[1::2])]
-            value = received[0]
-        return value
+    mine_index = (x * 4 + z) * 8 + y * 2 + core
+    sum_sent = []
+
+    def global_sum(which, value):
+        rows[which] = value
+        slots[which, mine_index] = value
+        for offsets in EVERY:
+            pltpu.make_async_remote_copy(src_ref=rows.at[which], dst_ref=slots.at[which, mine_index], send_sem=sum_send.at[which], recv_sem=sum_recv.at[which], device_id=peer(*offsets), device_id_type=MESH).start()
+        block = slots.at[which, pl.ds(0, len(EVERY))]
+        total = pltpu.make_async_remote_copy(src_ref=block, dst_ref=block, send_sem=sum_send.at[which], recv_sem=sum_recv.at[which], device_id=partner, device_id_type=MESH)
+        total.wait_recv()
+        sum_sent.append(total)
+        received = [slots[which, slot] for slot in range(DEVICES)]
+        while len(received) > 1:
+            received = [left + right for left, right in zip(received[::2], received[1::2])]
+        return received[0]
 
     grad_sq = global_sum(0, jnp.sum(fold(columns_loop(gather_sum, zero)), axis=0, keepdims=True))
     norm_sq = jnp.sum(grad_sq, axis=1, keepdims=True) / (REPLICAS * REPLICAS)
@@ -244,7 +266,7 @@
         block = row - 12 * layer
         return 4 * layer + jnp.where(block >= 3, 1, 0) + jnp.where(block >= 4, 1, 0) + jnp.where(block >= 8, 1, 0)
 
-    row_sums = jnp.broadcast_to(global_sum(len(SUM_ROUNDS), jnp.sum(spread_sums, axis=0, keepdims=True)), (8, 128))
+    row_sums = jnp.broadcast_to(global_sum(1, jnp.sum(spread_sums, axis=0, keepdims=True)), (8, 128))
     rate = []
     for tile in range(TILES):
         tensor = tensor_of(8 * tile + sub)
@@ -330,7 +352,7 @@
             hand(2, db, half)
     for copy in handed:
         copy.wait_recv()
-    for copy in started:
+    for copy in started + sum_sent:
         copy.wait_send()
 
 
@@ -387,11 +409,14 @@
                 slabs((), jnp.float32),
                 slabs((), jnp.float32),
                 slabs((), jnp.float32),
-                pltpu.VMEM((2 * len(SUM_ROUNDS), 1, 128), jnp.float32),
-                pltpu.VMEM((2 * len(SUM_ROUNDS), SLOTS, 1, 128), jnp.float32),
+                pltpu.VMEM((2, 1, 128), jnp.float32),
+                pltpu.VMEM((2, DEVICES, 1, 128), jnp.float32),
                 pltpu.SemaphoreType.DMA((COPIES,)),
                 pltpu.SemaphoreType.DMA((COPIES,)),
                 pltpu.SemaphoreType.DMA((LOADS,)),
+                pltpu.SemaphoreType.DMA((2,)),
+                pltpu.SemaphoreType.DMA((2,)),
+                pltpu.SemaphoreType.REGULAR((len(STAGES),)),
             ],
             compiler_params=pltpu.CompilerParams(collective_id=0, has_side_effects=True, vmem_limit_bytes=VMEM_LIMIT),
         )(*(pltpu.with_memory_space_constraint(operand, pltpu.HBM) for operand in operands))

time: 92.3 us -> 87.5 us (0.948)
  Pallas kernels: 91.5 us -> 86.7 us
    pallas_call x1, Pallas kernels: 88.1 us -> 83.3 us  [device_step(): pl.pallas_call(lamb_kernel, name='lamb_step', out_shape=(pltpu.VMEM((TILE...]
where the time goes in v4:
time: 87.5 us; the launch traced here: 87.3 us
  Pallas kernels  86.7 us (99%)
    pallas_call x1, Pallas kernels, device_step(): pl.pallas_call(lamb_kernel, name='lamb_step', out_shape=(pltpu.VMEM((TILE...  83.3 us
    pallas_call x1, Pallas kernels, device_step(): pl.pallas_call(write_kernel, name='write_out', out_shape=tuple((pltpu.HBM...  3.42 us

profile of v4, /device:TPU:1, one launch (start us, length us, event | category | flops | bytes accessed | tf_op | source)
XLA Modules:
  0.0 87.3 jit_solution(3099466854013600063)
XLA Ops:
  0.6 83.3 %lamb_step.1 = (bf16[3,8,147456]{2,1,0:T(8,128)(2,1)S(1)}, f32[3,8,4608]{2,1,0:T(8,128)S(1)}, f32[3,8,4608]{2,1,0:T(8,128)S(1)}, f32[3,8,4608]{2,1,0:T(8,128)S(1)}) custom-call(bf16[3,8,147456]{2,1,0:T(8,128)(2,1)} %bitcast.8, f32[3,8,4608]{2,1,0:T(8,128)} %bitcast.9, f32[3,8,4608]{2,1,0:T(8,128)} %bitcast.10, f32[3,8,4608]{2,1,0:T(8,128)} %bitcast.11), custom_call_target="tpu_custom_call" | custom-call | tf_op jit(solution)/shard_map/lamb_step/pallas_call | solution.py:386
  83.9 3.4 %write_out.1 = (bf16[3,8,147456]{2,1,0:T(8,128)(2,1)}, f32[3,8,4608]{2,1,0:T(8,128)}, f32[3,8,4608]{2,1,0:T(8,128)}, f32[3,8,4608]{2,1,0:T(8,128)}) custom-call(bf16[3,8,147456]{2,1,0:T(8,128)(2,1)S(1)} %get-tuple-element.12.params, f32[3,8,4608]{2,1,0:T(8,128)S(1)} %get-tuple-element.13.master, f32[3,8,4608]{2,1,0:T(8,128)S(1)} %get-tuple-element.14.one, ...), custom_call_target="tpu_custom_call" | custom-call | tf_op jit(solution)/shard_map/write_out/pallas_call | solution.py:423

commit v5 on v4

--- a/solution.py
+++ b/solution.py
@@ -21,6 +21,7 @@
 TILES = 3
 SLAB = 4608
 HALF = SLAB // 2
+QUARTER = SLAB // 4
 STEP_COLS = 768
 REPLICAS = 32
 LATE = (((2, 0), (1, 1), (1, 0), (0, 0)), ((2, 1), (3, 0), (3, 1), (0, 1)))
@@ -35,16 +36,19 @@
 OTHER_CORE = ((0, 0, 0, 1),)
 BARRIER = ALONG_X + ALONG_Z + ALONG_Y + OTHER_CORE + tuple((0, k, 0, 1) for k in (1, 3)) + tuple((0, 0, k, 1) for k in (1, 3))
 STAGES = (ALONG_X, OTHER_CORE, ALONG_Y, ALONG_Y, ALONG_Z, ALONG_Z)
-COPIES = 120
+GROUPS = ('raw', 'pair', 'early', 'late', 'mid', 'end', 'weight', 'step', 'gather')
+AHEAD = ('weight', 'step')
+COPIES = 82
 LOADS = len(ORDER) + 3
 VMEM_LIMIT = 40 * 2 ** 20
 WRITE_PIECES = 4
 
 
-def lamb_kernel(grads, master_in, one_in, two_in, params, master_out, one_out, two_out, own_raw, pair_raw, relay_raw, early, late, fin, sums, mid, end, master, one, two, grad_sum, direction, rows, slots, send_sem, recv_sem, load_sem, sum_send, sum_recv, stage_sem):
+def lamb_kernel(grads, master_in, one_in, two_in, params, master_out, one_out, two_out, own_raw, pair_raw, relay_raw, early, late, fin, sums, mid, end, master, one, two, grad_sum, direction, ahead_weight, ahead_step, rows, slots, send_sem, recv_sem, load_sem, sum_send, sum_recv, hand_sems, stage_sem):
     x, data = lax.axis_index('model'), lax.axis_index('data')
     core, y, z = lax.rem(data, 2), lax.rem(data // 2, 4), data // 8
     started = []
+    gathered = []
     loads = []
 
     def peer(dx, dz, dy, dc):
@@ -77,12 +81,19 @@
     def part(ref, half):
         return ref.at[:, :, pl.ds(half * HALF, HALF)]
 
-    def remote(src, dst, device):
-        index = len(started)
-        copy = pltpu.make_async_remote_copy(src_ref=src, dst_ref=dst, send_sem=send_sem.at[index], recv_sem=recv_sem.at[index], device_id=device, device_id_type=MESH)
+    def remote(src, dst, device, group='gather', landing=None):
+        if landing is None:
+            landing = recv_sem.at[len(started)]
+            started.append(group)
+        if group == 'gather':
+            gathered.append(src.shape[-1])
+        copy = pltpu.make_async_remote_copy(src_ref=src, dst_ref=dst, send_sem=send_sem.at[GROUPS.index(group)], recv_sem=landing, device_id=device, device_id_type=MESH)
         copy.start()
-        started.append(copy)
         return copy
+
+    def all_of(ref, group='gather', landing=None):
+        landing = recv_sem.at[0] if landing is None else landing
+        return pltpu.make_async_remote_copy(src_ref=ref, dst_ref=ref, send_sem=send_sem.at[GROUPS.index(group)], recv_sem=landing, device_id=partner, device_id_type=MESH)
 
     def load(src, dst):
         copy = pltpu.make_async_copy(src, dst, load_sem.at[len(loads)])
@@ -133,8 +144,8 @@
         for side in (0, 1):
             for other in (0, 1):
                 db, half = LATE[side][index]
-                raw_copy[side, other, index] = remote(piece(grads, 2, db, half, other), relay_raw.at[side, other, index], ring_a(side, other))
-    pair_copy = {key: remote(whole(grads, *key, other=1), pair_raw.at[place[key]], partner) for key in ORDER}
+                raw_copy[side, other, index] = remote(piece(grads, 2, db, half, other), relay_raw.at[side, other, index], ring_a(side, other), 'raw')
+    pair_copy = {key: remote(whole(grads, *key, other=1), pair_raw.at[place[key]], partner, 'pair') for key in ORDER}
 
     stage_signal(0)
 
@@ -167,7 +178,7 @@
         for side in (0, 1):
             db, half = EARLY[side][index]
             add_half(early.at[side, index], 0, pair_terms(1 + 2 * side, db, half))
-            fin_copy[side, db, half] = remote(early.at[side, index], part(fin.at[side, db], half), ring_a(side))
+            fin_copy[side, db, half] = remote(early.at[side, index], part(fin.at[side, db], half), ring_a(side), 'early')
         stage_next(index)
     for index in range(PIECES):
         for side in (0, 1):
@@ -177,7 +188,7 @@
                 raw_copy[side, other, index].wait_recv()
                 terms.append((relay_raw.at[side, other, index], 0))
             add_half(late.at[side, index], 0, terms)
-            fin_copy[side, db, half] = remote(late.at[side, index], part(fin.at[side, db], half), ring_a(side))
+            fin_copy[side, db, half] = remote(late.at[side, index], part(fin.at[side, db], half), ring_a(side), 'late')
         if PIECES + index < len(STAGES):
             stage_next(PIECES + index)
 
@@ -192,18 +203,21 @@
     end_copy = {}
     for side in (0, 1):
         first_sum(2, side)
-        mid_copy[side] = remote(part(sums.at[2], side), mid.at[side], ring_b(side))
+        mid_copy[side] = remote(part(sums.at[2], side), mid.at[side], ring_b(side), 'mid')
     for side in (0, 1):
         db, half = 1 + 2 * side, 1 - side
         first_sum(db, half)
-        end_copy[side, half] = remote(part(sums.at[db], half), part(end.at[side], half), ring_b(side))
+        end_copy[side, half] = remote(part(sums.at[db], half), part(end.at[side], half), ring_b(side), 'end')
     for side in (0, 1):
         first_sum(1 + 2 * side, side)
     for side in (0, 1):
         db = 1 + 2 * side
         mid_copy[side].wait_recv()
         add_half(sums.at[db], side * HALF, [(sums.at[db], side * HALF), (mid.at[side], 0)])
-        end_copy[side, side] = remote(part(sums.at[db], side), part(end.at[side], side), ring_b(side))
+        end_copy[side, side] = remote(part(sums.at[db], side), part(end.at[side], side), ring_b(side), 'end')
+    ahead_copy = {}
+    for side in (0, 1):
+        ahead_copy[2, side] = remote(part(master, 0), part(ahead_weight.at[side], 0), ring_b(side), 'weight')
     for side in (0, 1):
         first_sum(0, side)
     for side in (0, 1):
@@ -221,11 +235,13 @@
     mine_index = (x * 4 + z) * 8 + y * 2 + core
     sum_sent = []
 
-    def global_sum(which, value):
+    def global_sum(which, value, source, target):
         rows[which] = value
         slots[which, mine_index] = value
         for offsets in EVERY:
             pltpu.make_async_remote_copy(src_ref=rows.at[which], dst_ref=slots.at[which, mine_index], send_sem=sum_send.at[which], recv_sem=sum_recv.at[which], device_id=peer(*offsets), device_id_type=MESH).start()
+        for side in (0, 1):
+            ahead_copy[which, side] = remote(source, target(side), ring_b(side), AHEAD[which])
         block = slots.at[which, pl.ds(0, len(EVERY))]
         total = pltpu.make_async_remote_copy(src_ref=block, dst_ref=block, send_sem=sum_send.at[which], recv_sem=sum_recv.at[which], device_id=partner, device_id_type=MESH)
         total.wait_recv()
@@ -235,7 +251,7 @@
             received = [left + right for left, right in zip(received[::2], received[1::2])]
         return received[0]
 
-    grad_sq = global_sum(0, jnp.sum(fold(columns_loop(gather_sum, zero)), axis=0, keepdims=True))
+    grad_sq = global_sum(0, jnp.sum(fold(columns_loop(gather_sum, zero)), axis=0, keepdims=True), part(master, 1), lambda side: part(ahead_weight.at[side], 1))
     norm_sq = jnp.sum(grad_sq, axis=1, keepdims=True) / (REPLICAS * REPLICAS)
     clip = jnp.minimum(1.0, MAX_NORM / jnp.sqrt(norm_sq)) / REPLICAS
 
@@ -266,7 +282,7 @@
         block = row - 12 * layer
         return 4 * layer + jnp.where(block >= 3, 1, 0) + jnp.where(block >= 4, 1, 0) + jnp.where(block >= 8, 1, 0)
 
-    row_sums = jnp.broadcast_to(global_sum(1, jnp.sum(spread_sums, axis=0, keepdims=True)), (8, 128))
+    row_sums = jnp.broadcast_to(global_sum(1, jnp.sum(spread_sums, axis=0, keepdims=True), direction, lambda side: ahead_step.at[side]), (8, 128))
     rate = []
     for tile in range(TILES):
         tensor = tensor_of(8 * tile + sub)
@@ -276,19 +292,21 @@
         weight_norm = jnp.sqrt(jnp.sum(jnp.where(weight_mask, row_sums, 0.0), axis=1, keepdims=True))
         rate.append(LEARN_RATE * (weight_norm / step_norm))
 
-    own_column = column(0, 0)
-
-    def weights(offset, carry):
-        for tile in range(TILES):
-            value = master[tile, :, at(offset)] - rate[tile] * direction[tile, :, at(offset)]
-            master_out[tile, :, at(offset)] = value
-            params[tile, :, at(own_column + offset)] = value.astype(jnp.bfloat16)
-        return carry
-
-    columns_loop(weights)
+    def weights(db, weight, step, master_new=None):
+        start = column(0, db)
+
+        def body(offset, carry):
+            for tile in range(TILES):
+                value = weight[tile, :, at(offset)] - rate[tile] * step[tile, :, at(offset)]
+                if master_new is not None:
+                    master_new[tile, :, at(offset)] = value
+                params[tile, :, at(start + offset)] = value.astype(jnp.bfloat16)
+            return carry
+
+        columns_loop(body)
 
     handed = []
-    along_b = {}
+    hand_sem = hand_sems.at[0]
     along_a = {}
     far_b = {}
     far_a = {}
@@ -297,63 +315,76 @@
         ref = piece(params, da, db, half)
         return remote(ref, ref, device)
 
+    def give(ref, device):
+        handed.append(ref.shape[-1])
+        remote(ref, ref, device, 'gather', hand_sem)
+
     def hand(da, db, half):
-        handed.append(send(da, db, half, partner))
+        give(piece(params, da, db, half), partner)
 
     def pass_on(first, second):
         for one_piece, other_piece in ((first, second), (second, first)):
             along_a[0, one_piece] = send(0, *one_piece, ring_a(0))
             along_a[1, other_piece] = send(0, *other_piece, ring_a(1))
 
-    for order in (0, 1):
-        for side in (0, 1):
-            half = side if order == 0 else 1 - side
-            along_b[side, half] = send(0, 0, half, ring_b(side))
-        for side in (0, 1):
-            half = side if order == 0 else 1 - side
-            along_a[side, (0, half)] = send(0, 0, half, ring_a(side))
-    hand(0, 0, 0)
-    hand(0, 0, 1)
+    def quarter(da, half, index):
+        start = column(da, 2) + half * HALF + index * QUARTER
+        return params.at[:, :, pl.ds(pl.multiple_of(start, QUARTER), QUARTER)]
 
     def arrived(side, db, half):
         along_a[side, (db, half)].wait_recv()
         da = 3 - 2 * side
-        if half == side:
+        if half == side and db == 2:
+            first, second = quarter(da, half, 0), quarter(da, half, 1)
+            far_a[db, half] = remote(first, first, ring_a(side))
+            give(second, ring_a(side))
+            give(second, peer(0, (1 - 2 * side) * core, (1 - 2 * side) * (1 - core), 1))
+        elif half == side:
             far_a[db, half] = send(da, db, half, ring_a(side))
         hand(da, db, half)
 
+    weights(0, master, direction, master_out)
+    pass_on((0, 0), (0, 1))
+    hand(0, 0, 0)
+    hand(0, 0, 1)
     for side in (0, 1):
         db = 3 - 2 * side
-        along_b[side, side].wait_recv()
+        for which in (2, 0, 1):
+            ahead_copy[which, side].wait_recv()
+        weights(db, ahead_weight.at[side], ahead_step.at[side])
         far_b[side] = send(0, db, side, ring_b(side))
     pass_on((3, 0), (1, 1))
-    hand(0, 3, 0)
-    hand(0, 1, 1)
+    pass_on((1, 0), (3, 1))
+    for half in (0, 1):
+        hand(0, 3, half)
+        hand(0, 1, 1 - half)
     for side in (0, 1):
         arrived(side, 0, side)
-    for side in (0, 1):
-        along_b[side, 1 - side].wait_recv()
-    pass_on((1, 0), (3, 1))
-    hand(0, 3, 1)
-    hand(0, 1, 0)
-    for side in (0, 1):
-        arrived(side, 0, 1 - side)
     for side in (0, 1):
         far_b[side].wait_recv()
     pass_on((2, 0), (2, 1))
     hand(0, 2, 0)
     hand(0, 2, 1)
+    for ref, group in ((relay_raw, 'raw'), (pair_raw, 'pair'), (early, 'early'), (late, 'late'), (mid, 'mid'), (end, 'end'), (ahead_weight, 'weight'), (ahead_step, 'step')):
+        all_of(ref, group).wait_send()
+    for copy in sum_sent:
+        copy.wait_send()
+    for side in (0, 1):
+        arrived(side, 0, 1 - side)
     for pieces in (((3, 0), (1, 1)), ((1, 1), (3, 0)), ((1, 0), (3, 1)), ((3, 1), (1, 0)), ((2, 0), (2, 1)), ((2, 1), (2, 0))):
         for side in (0, 1):
             arrived(side, *pieces[side])
     for db in (0, 3, 1, 2):
         for half in (0, 1):
             far_a[db, half].wait_recv()
-            hand(2, db, half)
-    for copy in handed:
-        copy.wait_recv()
-    for copy in started + sum_sent:
-        copy.wait_send()
+            if db == 2:
+                give(quarter(2, half, 0), partner)
+            else:
+                hand(2, db, half)
+    if len(started) != COPIES:
+        raise ValueError(len(started))
+    all_of(params.at[:, :, pl.ds(0, sum(handed))], landing=hand_sem).wait_recv()
+    all_of(params.at[:, :, pl.ds(0, sum(gathered))]).wait_send()
 
 
 def write_kernel(params, master, one, two, params_out, master_out, one_out, two_out, sem):
@@ -409,13 +440,16 @@
                 slabs((), jnp.float32),
                 slabs((), jnp.float32),
                 slabs((), jnp.float32),
+                slabs((2,), jnp.float32),
+                slabs((2,), jnp.float32),
                 pltpu.VMEM((2, 1, 128), jnp.float32),
                 pltpu.VMEM((2, DEVICES, 1, 128), jnp.float32),
-                pltpu.SemaphoreType.DMA((COPIES,)),
+                pltpu.SemaphoreType.DMA((len(GROUPS),)),
                 pltpu.SemaphoreType.DMA((COPIES,)),
                 pltpu.SemaphoreType.DMA((LOADS,)),
                 pltpu.SemaphoreType.DMA((2,)),
                 pltpu.SemaphoreType.DMA((2,)),
+                pltpu.SemaphoreType.DMA((1,)),
                 pltpu.SemaphoreType.REGULAR((len(STAGES),)),
             ],
             compiler_params=pltpu.CompilerParams(collective_id=0, has_side_effects=True, vmem_limit_bytes=VMEM_LIMIT),

time: 87.5 us -> 83.8 us (0.958)
  Pallas kernels: 86.7 us -> 83.1 us
    pallas_call x1, Pallas kernels: 83.3 us -> 79.7 us  [device_step(): pl.pallas_call(lamb_kernel, name='lamb_step', out_shape=(pltpu.VMEM((TILE...]
where the time goes in v5:
time: 83.8 us; the launch traced here: 83.7 us
  Pallas kernels  83.1 us (99%)
    pallas_call x1, Pallas kernels, device_step(): pl.pallas_call(lamb_kernel, name='lamb_step', out_shape=(pltpu.VMEM((TILE...  79.7 us
    pallas_call x1, Pallas kernels, device_step(): pl.pallas_call(write_kernel, name='write_out', out_shape=tuple((pltpu.HBM...  3.42 us

profile of v5, /device:TPU:1, one launch (start us, length us, event | category | flops | bytes accessed | tf_op | source)
XLA Modules:
  0.0 83.7 jit_solution(6013749755533340314)
XLA Ops:
  0.6 79.7 %lamb_step.1 = (bf16[3,8,147456]{2,1,0:T(8,128)(2,1)S(1)}, f32[3,8,4608]{2,1,0:T(8,128)S(1)}, f32[3,8,4608]{2,1,0:T(8,128)S(1)}, f32[3,8,4608]{2,1,0:T(8,128)S(1)}) custom-call(bf16[3,8,147456]{2,1,0:T(8,128)(2,1)} %bitcast.8, f32[3,8,4608]{2,1,0:T(8,128)} %bitcast.9, f32[3,8,4608]{2,1,0:T(8,128)} %bitcast.10, f32[3,8,4608]{2,1,0:T(8,128)} %bitcast.11), custom_call_target="tpu_custom_call" | custom-call | tf_op jit(solution)/shard_map/lamb_step/pallas_call | solution.py:417
  80.3 3.4 %write_out.1 = (bf16[3,8,147456]{2,1,0:T(8,128)(2,1)}, f32[3,8,4608]{2,1,0:T(8,128)}, f32[3,8,4608]{2,1,0:T(8,128)}, f32[3,8,4608]{2,1,0:T(8,128)}) custom-call(bf16[3,8,147456]{2,1,0:T(8,128)(2,1)S(1)} %get-tuple-element.12.params, f32[3,8,4608]{2,1,0:T(8,128)S(1)} %get-tuple-element.13.master, f32[3,8,4608]{2,1,0:T(8,128)S(1)} %get-tuple-element.14.one, ...), custom_call_target="tpu_custom_call" | custom-call | tf_op jit(solution)/shard_map/write_out/pallas_call | solution.py:457

commit v6 on v5

--- a/solution.py
+++ b/solution.py
@@ -38,18 +38,18 @@
 STAGES = (ALONG_X, OTHER_CORE, ALONG_Y, ALONG_Y, ALONG_Z, ALONG_Z)
 GROUPS = ('raw', 'pair', 'early', 'late', 'mid', 'end', 'weight', 'step', 'gather')
 AHEAD = ('weight', 'step')
-COPIES = 82
-LOADS = len(ORDER) + 3
+COPIES = 36
+BATCH = 4
 VMEM_LIMIT = 40 * 2 ** 20
 WRITE_PIECES = 4
 
 
-def lamb_kernel(grads, master_in, one_in, two_in, params, master_out, one_out, two_out, own_raw, pair_raw, relay_raw, early, late, fin, sums, mid, end, master, one, two, grad_sum, direction, ahead_weight, ahead_step, rows, slots, send_sem, recv_sem, load_sem, sum_send, sum_recv, hand_sems, stage_sem):
+def lamb_kernel(grads, master_in, one_in, two_in, params, master_out, one_out, two_out, own_raw, pair_raw, relay_raw, early, late, fin, sums, mid, end, state, grad_sum, direction, ahead_weight, ahead_step, rows, slots, send_sem, recv_sem, sum_send, sum_recv, group_sem, raw_sem, pair_sem, ahead_sem, stage_sem):
     x, data = lax.axis_index('model'), lax.axis_index('data')
     core, y, z = lax.rem(data, 2), lax.rem(data // 2, 4), data // 8
     started = []
     gathered = []
-    loads = []
+    hand_sem, own_sem, state_sem, early_sem, end_sem = (group_sem.at[index] for index in range(5))
 
     def peer(dx, dz, dy, dc):
         chip = lax.rem(z + dz + 4, 4) * 4 + lax.rem(y + dy + 4, 4)
@@ -95,11 +95,8 @@
         landing = recv_sem.at[0] if landing is None else landing
         return pltpu.make_async_remote_copy(src_ref=ref, dst_ref=ref, send_sem=send_sem.at[GROUPS.index(group)], recv_sem=landing, device_id=partner, device_id_type=MESH)
 
-    def load(src, dst):
-        copy = pltpu.make_async_copy(src, dst, load_sem.at[len(loads)])
-        copy.start()
-        loads.append(copy)
-        return copy
+    def load(src, dst, sem):
+        pltpu.make_async_copy(src, dst, sem).start()
 
     def columns_loop(body, init=0, length=SLAB):
         def step(index, carry):
@@ -134,18 +131,21 @@
             stage_signal(stage + 1)
 
     place = {key: index for index, key in enumerate(ORDER)}
-    own_load = {key: load(whole(grads, *key), own_raw.at[place[key]]) for key in ORDER}
-    state_load = [load(src, dst) for src, dst in ((master_in, master), (one_in, one), (two_in, two))]
+    for key in ORDER:
+        load(whole(grads, *key), own_raw.at[place[key]], own_sem)
+    for index, source in enumerate((master_in, one_in, two_in)):
+        load(source, state.at[index], state_sem)
+    master, one, two = (state.at[index] for index in range(3))
 
     pl.semaphore_wait(barrier, len(BARRIER))
 
-    raw_copy = {}
     for index in range(PIECES):
         for side in (0, 1):
             for other in (0, 1):
                 db, half = LATE[side][index]
-                raw_copy[side, other, index] = remote(piece(grads, 2, db, half, other), relay_raw.at[side, other, index], ring_a(side, other), 'raw')
-    pair_copy = {key: remote(whole(grads, *key, other=1), pair_raw.at[place[key]], partner, 'pair') for key in ORDER}
+                remote(piece(grads, 2, db, half, other), relay_raw.at[side, other, index], ring_a(side, other), 'raw', raw_sem.at[side, index])
+    for key in ORDER:
+        remote(whole(grads, *key, other=1), pair_raw.at[place[key]], partner, 'pair', pair_sem.at[place[key] // BATCH])
 
     stage_signal(0)
 
@@ -158,72 +158,73 @@
     def weight_square(offset, carry):
         return tuple(carry[tile] + master[tile, :, at(offset)] * master[tile, :, at(offset)] for tile in range(TILES))
 
-    for copy in state_load:
-        copy.wait()
+    pltpu.make_async_copy(state, state, state_sem).wait()
     zero = jnp.zeros((8, STEP_COLS), jnp.float32)
     weight_sq = [jnp.sum(fold(value), axis=1, keepdims=True) for value in columns_loop(weight_square, (zero,) * TILES)]
 
     ready = set()
 
     def pair_terms(da, db, half):
-        key = (da, db)
-        if key not in ready:
-            own_load[key].wait()
-            pair_copy[key].wait_recv()
-            ready.add(key)
-        return [(own_raw.at[place[key]], half * HALF), (pair_raw.at[place[key]], half * HALF)]
+        slot = place[da, db]
+        batch = slot // BATCH
+        if not ready:
+            pltpu.make_async_copy(own_raw, own_raw, own_sem).wait()
+        if batch not in ready:
+            all_of(pair_raw.at[pl.ds(batch * BATCH, BATCH)], 'pair', pair_sem.at[batch]).wait_recv()
+            ready.add(batch)
+        return [(own_raw.at[slot], half * HALF), (pair_raw.at[slot], half * HALF)]
 
     fin_copy = {}
     for index in range(PIECES):
         for side in (0, 1):
             db, half = EARLY[side][index]
             add_half(early.at[side, index], 0, pair_terms(1 + 2 * side, db, half))
-            fin_copy[side, db, half] = remote(early.at[side, index], part(fin.at[side, db], half), ring_a(side), 'early')
+            remote(early.at[side, index], part(fin.at[side, db], half), ring_a(side), 'early', early_sem)
         stage_next(index)
     for index in range(PIECES):
         for side in (0, 1):
             db, half = LATE[side][index]
             terms = pair_terms(1 + 2 * side, db, half)
-            for other in (0, 1):
-                raw_copy[side, other, index].wait_recv()
-                terms.append((relay_raw.at[side, other, index], 0))
+            all_of(relay_raw.at[side, pl.ds(0, 2), index], 'raw', raw_sem.at[side, index]).wait_recv()
+            terms += [(relay_raw.at[side, other, index], 0) for other in (0, 1)]
             add_half(late.at[side, index], 0, terms)
             fin_copy[side, db, half] = remote(late.at[side, index], part(fin.at[side, db], half), ring_a(side), 'late')
         if PIECES + index < len(STAGES):
             stage_next(PIECES + index)
 
+    arrived_early = []
+
     def first_sum(db, half):
         terms = pair_terms(0, db, half)
-        for side in (0, 1):
-            fin_copy[side, db, half].wait_recv()
+        if not arrived_early:
+            all_of(early, 'early', early_sem).wait_recv()
+            arrived_early.append(db)
+        for side in (0, 1):
+            if (side, db, half) in fin_copy:
+                fin_copy[side, db, half].wait_recv()
             terms.append((fin.at[side, db], half * HALF))
         add_half(sums.at[db], half * HALF, terms)
 
     mid_copy = {}
-    end_copy = {}
     for side in (0, 1):
         first_sum(2, side)
         mid_copy[side] = remote(part(sums.at[2], side), mid.at[side], ring_b(side), 'mid')
     for side in (0, 1):
         db, half = 1 + 2 * side, 1 - side
         first_sum(db, half)
-        end_copy[side, half] = remote(part(sums.at[db], half), part(end.at[side], half), ring_b(side), 'end')
+        remote(part(sums.at[db], half), part(end.at[side], half), ring_b(side), 'end', end_sem)
     for side in (0, 1):
         first_sum(1 + 2 * side, side)
     for side in (0, 1):
         db = 1 + 2 * side
         mid_copy[side].wait_recv()
         add_half(sums.at[db], side * HALF, [(sums.at[db], side * HALF), (mid.at[side], 0)])
-        end_copy[side, side] = remote(part(sums.at[db], side), part(end.at[side], side), ring_b(side), 'end')
-    ahead_copy = {}
-    for side in (0, 1):
-        ahead_copy[2, side] = remote(part(master, 0), part(ahead_weight.at[side], 0), ring_b(side), 'weight')
+        remote(part(sums.at[db], side), part(end.at[side], side), ring_b(side), 'end', end_sem)
+    for side in (0, 1):
+        remote(part(master, 0), part(ahead_weight.at[side], 0), ring_b(side), 'weight', ahead_sem.at[0])
     for side in (0, 1):
         first_sum(0, side)
-    for side in (0, 1):
-        end_copy[side, 1 - side].wait_recv()
-    for side in (0, 1):
-        end_copy[side, side].wait_recv()
+    all_of(end, 'end', end_sem).wait_recv()
 
     def gather_sum(offset, carry):
         for tile in range(TILES):
@@ -241,7 +242,7 @@
         for offsets in EVERY:
             pltpu.make_async_remote_copy(src_ref=rows.at[which], dst_ref=slots.at[which, mine_index], send_sem=sum_send.at[which], recv_sem=sum_recv.at[which], device_id=peer(*offsets), device_id_type=MESH).start()
         for side in (0, 1):
-            ahead_copy[which, side] = remote(source, target(side), ring_b(side), AHEAD[which])
+            remote(source, target(side), ring_b(side), AHEAD[which], ahead_sem.at[which])
         block = slots.at[which, pl.ds(0, len(EVERY))]
         total = pltpu.make_async_remote_copy(src_ref=block, dst_ref=block, send_sem=sum_send.at[which], recv_sem=sum_recv.at[which], device_id=partner, device_id_type=MESH)
         total.wait_recv()
@@ -306,7 +307,6 @@
         columns_loop(body)
 
     handed = []
-    hand_sem = hand_sems.at[0]
     along_a = {}
     far_b = {}
     far_a = {}
@@ -347,10 +347,10 @@
     pass_on((0, 0), (0, 1))
     hand(0, 0, 0)
     hand(0, 0, 1)
+    all_of(ahead_weight, 'weight', ahead_sem.at[0]).wait_recv()
+    all_of(ahead_step, 'step', ahead_sem.at[1]).wait_recv()
     for side in (0, 1):
         db = 3 - 2 * side
-        for which in (2, 0, 1):
-            ahead_copy[which, side].wait_recv()
         weights(db, ahead_weight.at[side], ahead_step.at[side])
         far_b[side] = send(0, db, side, ring_b(side))
     pass_on((3, 0), (1, 1))
@@ -393,12 +393,13 @@
     for tile in range(TILES):
         for index in range(WRITE_PIECES):
             cols = pl.ds(index * width, width)
-            pairs.append((params.at[tile, :, cols], params_out.at[tile, :, cols]))
-    copies = [pltpu.make_async_copy(src, dst, sem.at[index]) for index, (src, dst) in enumerate(pairs)]
+            pltpu.make_async_copy(params.at[tile, :, cols], params_out.at[tile, :, cols], sem.at[0]).start()
+    copies = [pltpu.make_async_copy(src, dst, sem.at[1 + index]) for index, (src, dst) in enumerate(pairs)]
     for copy in copies:
         copy.start()
     for copy in copies:
         copy.wait()
+    pltpu.make_async_copy(params, params_out, sem.at[0]).wait()
 
 
 def solution(mesh):
@@ -435,9 +436,7 @@
                 slabs((4,), jnp.float32),
                 slabs((2,), jnp.float32, HALF),
                 slabs((2,), jnp.float32),
-                slabs((), jnp.float32),
-                slabs((), jnp.float32),
-                slabs((), jnp.float32),
+                slabs((3,), jnp.float32),
                 slabs((), jnp.float32),
                 slabs((), jnp.float32),
                 slabs((2,), jnp.float32),
@@ -446,10 +445,12 @@
                 pltpu.VMEM((2, DEVICES, 1, 128), jnp.float32),
                 pltpu.SemaphoreType.DMA((len(GROUPS),)),
                 pltpu.SemaphoreType.DMA((COPIES,)),
-                pltpu.SemaphoreType.DMA((LOADS,)),
                 pltpu.SemaphoreType.DMA((2,)),
                 pltpu.SemaphoreType.DMA((2,)),
-                pltpu.SemaphoreType.DMA((1,)),
+                pltpu.SemaphoreType.DMA((5,)),
+                pltpu.SemaphoreType.DMA((2, PIECES)),
+                pltpu.SemaphoreType.DMA((len(ORDER) // BATCH,)),
+                pltpu.SemaphoreType.DMA((2,)),
                 pltpu.SemaphoreType.REGULAR((len(STAGES),)),
             ],
             compiler_params=pltpu.CompilerParams(collective_id=0, has_side_effects=True, vmem_limit_bytes=VMEM_LIMIT),
@@ -460,7 +461,7 @@
             out_shape=tuple(pltpu.HBM(result.shape, result.dtype) for result in results),
             in_specs=[vmem] * 4,
             out_specs=(hbm,) * 4,
-            scratch_shapes=[pltpu.SemaphoreType.DMA((TILES * WRITE_PIECES + 3,))],
+            scratch_shapes=[pltpu.SemaphoreType.DMA((4,))],
             compiler_params=pltpu.CompilerParams(vmem_limit_bytes=2 ** 20),
         )(*results)
         return tuple(out.reshape(24, -1) for out in outs)

time: 83.8 us -> 83.4 us (level)
  no operation moved by 1% of the time
where the time goes in v6:
time: 83.4 us; the launch traced here: 83.2 us
  Pallas kernels  82.6 us (99%)
    pallas_call x1, Pallas kernels, device_step(): pl.pallas_call(lamb_kernel, name='lamb_step', out_shape=(pltpu.VMEM((TILE...  79.3 us
    pallas_call x1, Pallas kernels, device_step(): pl.pallas_call(write_kernel, name='write_out', out_shape=tuple((pltpu.HBM...  3.33 us

profile of v6, /device:TPU:1, one launch (start us, length us, event | category | flops | bytes accessed | tf_op | source)
XLA Modules:
  0.0 83.2 jit_solution(2113714921274829374)
XLA Ops:
  0.6 79.3 %lamb_step.1 = (bf16[3,8,147456]{2,1,0:T(8,128)(2,1)S(1)}, f32[3,8,4608]{2,1,0:T(8,128)S(1)}, f32[3,8,4608]{2,1,0:T(8,128)S(1)}, f32[3,8,4608]{2,1,0:T(8,128)S(1)}) custom-call(bf16[3,8,147456]{2,1,0:T(8,128)(2,1)} %bitcast.8, f32[3,8,4608]{2,1,0:T(8,128)} %bitcast.9, f32[3,8,4608]{2,1,0:T(8,128)} %bitcast.10, f32[3,8,4608]{2,1,0:T(8,128)} %bitcast.11), custom_call_target="tpu_custom_call" | custom-call | tf_op jit(solution)/shard_map/lamb_step/pallas_call | solution.py:418
  79.9 3.3 %write_out.1 = (bf16[3,8,147456]{2,1,0:T(8,128)(2,1)}, f32[3,8,4608]{2,1,0:T(8,128)}, f32[3,8,4608]{2,1,0:T(8,128)}, f32[3,8,4608]{2,1,0:T(8,128)}) custom-call(bf16[3,8,147456]{2,1,0:T(8,128)(2,1)S(1)} %get-tuple-element.12.params, f32[3,8,4608]{2,1,0:T(8,128)S(1)} %get-tuple-element.13.master, f32[3,8,4608]{2,1,0:T(8,128)S(1)} %get-tuple-element.14.one, ...), custom_call_target="tpu_custom_call" | custom-call | tf_op jit(solution)/shard_map/write_out/pallas_call | solution.py:458

commit v7 on v6

--- a/solution.py
+++ b/solution.py
@@ -37,11 +37,10 @@
 BARRIER = ALONG_X + ALONG_Z + ALONG_Y + OTHER_CORE + tuple((0, k, 0, 1) for k in (1, 3)) + tuple((0, 0, k, 1) for k in (1, 3))
 STAGES = (ALONG_X, OTHER_CORE, ALONG_Y, ALONG_Y, ALONG_Z, ALONG_Z)
 GROUPS = ('raw', 'pair', 'early', 'late', 'mid', 'end', 'weight', 'step', 'gather')
-AHEAD = ('weight', 'step')
-COPIES = 36
+COPIES = 38
 BATCH = 4
 VMEM_LIMIT = 40 * 2 ** 20
-WRITE_PIECES = 4
+WRITE_PIECES = 2
 
 
 def lamb_kernel(grads, master_in, one_in, two_in, params, master_out, one_out, two_out, own_raw, pair_raw, relay_raw, early, late, fin, sums, mid, end, state, grad_sum, direction, ahead_weight, ahead_step, rows, slots, send_sem, recv_sem, sum_send, sum_recv, group_sem, raw_sem, pair_sem, ahead_sem, stage_sem):
@@ -131,21 +130,21 @@
             stage_signal(stage + 1)
 
     place = {key: index for index, key in enumerate(ORDER)}
+    pl.semaphore_wait(barrier, len(BARRIER))
+
+    for index in range(PIECES):
+        for side in (0, 1):
+            for other in (0, 1):
+                db, half = LATE[side][index]
+                remote(piece(grads, 2, db, half, other), relay_raw.at[side, other, index], ring_a(side, other), 'raw', raw_sem.at[side, index])
+    for key in ORDER:
+        remote(whole(grads, *key, other=1), pair_raw.at[place[key]], partner, 'pair', pair_sem.at[place[key] // BATCH])
+
     for key in ORDER:
         load(whole(grads, *key), own_raw.at[place[key]], own_sem)
     for index, source in enumerate((master_in, one_in, two_in)):
         load(source, state.at[index], state_sem)
     master, one, two = (state.at[index] for index in range(3))
-
-    pl.semaphore_wait(barrier, len(BARRIER))
-
-    for index in range(PIECES):
-        for side in (0, 1):
-            for other in (0, 1):
-                db, half = LATE[side][index]
-                remote(piece(grads, 2, db, half, other), relay_raw.at[side, other, index], ring_a(side, other), 'raw', raw_sem.at[side, index])
-    for key in ORDER:
-        remote(whole(grads, *key, other=1), pair_raw.at[place[key]], partner, 'pair', pair_sem.at[place[key] // BATCH])
 
     stage_signal(0)
 
@@ -221,7 +220,7 @@
         add_half(sums.at[db], side * HALF, [(sums.at[db], side * HALF), (mid.at[side], 0)])
         remote(part(sums.at[db], side), part(end.at[side], side), ring_b(side), 'end', end_sem)
     for side in (0, 1):
-        remote(part(master, 0), part(ahead_weight.at[side], 0), ring_b(side), 'weight', ahead_sem.at[0])
+        remote(part(master, side), part(ahead_weight.at[side], side), ring_b(side), 'weight', ahead_sem.at[0])
     for side in (0, 1):
         first_sum(0, side)
     all_of(end, 'end', end_sem).wait_recv()
@@ -236,13 +235,13 @@
     mine_index = (x * 4 + z) * 8 + y * 2 + core
     sum_sent = []
 
-    def global_sum(which, value, source, target):
+    def global_sum(which, value, meanwhile=None):
         rows[which] = value
         slots[which, mine_index] = value
         for offsets in EVERY:
             pltpu.make_async_remote_copy(src_ref=rows.at[which], dst_ref=slots.at[which, mine_index], send_sem=sum_send.at[which], recv_sem=sum_recv.at[which], device_id=peer(*offsets), device_id_type=MESH).start()
-        for side in (0, 1):
-            remote(source, target(side), ring_b(side), AHEAD[which], ahead_sem.at[which])
+        if meanwhile is not None:
+            meanwhile()
         block = slots.at[which, pl.ds(0, len(EVERY))]
         total = pltpu.make_async_remote_copy(src_ref=block, dst_ref=block, send_sem=sum_send.at[which], recv_sem=sum_recv.at[which], device_id=partner, device_id_type=MESH)
         total.wait_recv()
@@ -252,22 +251,34 @@
             received = [left + right for left, right in zip(received[::2], received[1::2])]
         return received[0]
 
-    grad_sq = global_sum(0, jnp.sum(fold(columns_loop(gather_sum, zero)), axis=0, keepdims=True), part(master, 1), lambda side: part(ahead_weight.at[side], 1))
+    grad_sq = global_sum(0, jnp.sum(fold(columns_loop(gather_sum, zero)), axis=0, keepdims=True))
     norm_sq = jnp.sum(grad_sq, axis=1, keepdims=True) / (REPLICAS * REPLICAS)
     clip = jnp.minimum(1.0, MAX_NORM / jnp.sqrt(norm_sq)) / REPLICAS
+
+    def new_moments(tile, cols):
+        scaled = clip * grad_sum[tile, :, cols]
+        new_one = BETA_ONE * one[tile, :, cols] + (1.0 - BETA_ONE) * scaled
+        new_two = BETA_TWO * two[tile, :, cols] + (1.0 - BETA_TWO) * scaled * scaled
+        return new_one, new_two
 
     def moments(offset, carry):
         squares = []
         for tile in range(TILES):
-            scaled = clip * grad_sum[tile, :, at(offset)]
-            new_one = BETA_ONE * one[tile, :, at(offset)] + (1.0 - BETA_ONE) * scaled
-            new_two = BETA_TWO * two[tile, :, at(offset)] + (1.0 - BETA_TWO) * scaled * scaled
+            new_one, new_two = new_moments(tile, at(offset))
             step = (new_one * (1.0 / CORR_ONE)) / (jnp.sqrt(new_two * (1.0 / CORR_TWO)) + EPSILON) + WEIGHT_DECAY * master[tile, :, at(offset)]
-            one_out[tile, :, at(offset)] = new_one
-            two_out[tile, :, at(offset)] = new_two
             direction[tile, :, at(offset)] = step
             squares.append(carry[tile] + step * step)
         return tuple(squares)
+
+    def store_moments():
+        for side in (0, 1):
+            remote(part(direction, side), part(ahead_step.at[side], side), ring_b(side), 'step', ahead_sem.at[1])
+
+        def body(offset, carry):
+            for tile in range(TILES):
+                one_out[tile, :, at(offset)], two_out[tile, :, at(offset)] = new_moments(tile, at(offset))
+            return carry
+        columns_loop(body)
 
     step_sq = [jnp.sum(fold(value), axis=1, keepdims=True) for value in columns_loop(moments, (zero,) * TILES)]
 
@@ -283,28 +294,28 @@
         block = row - 12 * layer
         return 4 * layer + jnp.where(block >= 3, 1, 0) + jnp.where(block >= 4, 1, 0) + jnp.where(block >= 8, 1, 0)
 
-    row_sums = jnp.broadcast_to(global_sum(1, jnp.sum(spread_sums, axis=0, keepdims=True), direction, lambda side: ahead_step.at[side]), (8, 128))
-    rate = []
+    masks = []
     for tile in range(TILES):
         tensor = tensor_of(8 * tile + sub)
-        step_mask = (tensor_of(lane) == tensor) & (lane < 24)
-        weight_mask = (tensor_of(lane - 32) == tensor) & (lane >= 32) & (lane < 56)
-        step_norm = jnp.sqrt(jnp.sum(jnp.where(step_mask, row_sums, 0.0), axis=1, keepdims=True))
-        weight_norm = jnp.sqrt(jnp.sum(jnp.where(weight_mask, row_sums, 0.0), axis=1, keepdims=True))
+        masks.append(((tensor_of(lane) == tensor) & (lane < 24), (tensor_of(lane - 32) == tensor) & (lane >= 32) & (lane < 56)))
+    row_sums = jnp.broadcast_to(global_sum(1, jnp.sum(spread_sums, axis=0, keepdims=True), store_moments), (8, 128))
+    rate = []
+    for step_mask, weight_mask in masks:
+        step_norm, weight_norm = (jnp.sqrt(jnp.sum(jnp.where(mask, row_sums, 0.0), axis=1, keepdims=True)) for mask in (step_mask, weight_mask))
         rate.append(LEARN_RATE * (weight_norm / step_norm))
 
-    def weights(db, weight, step, master_new=None):
+    def weights(db, weight, step, master_new=None, first=0, length=SLAB):
         start = column(0, db)
 
         def body(offset, carry):
             for tile in range(TILES):
-                value = weight[tile, :, at(offset)] - rate[tile] * step[tile, :, at(offset)]
+                value = weight[tile, :, at(first + offset)] - rate[tile] * step[tile, :, at(first + offset)]
                 if master_new is not None:
-                    master_new[tile, :, at(offset)] = value
-                params[tile, :, at(start + offset)] = value.astype(jnp.bfloat16)
+                    master_new[tile, :, at(first + offset)] = value
+                params[tile, :, at(start + first + offset)] = value.astype(jnp.bfloat16)
             return carry
 
-        columns_loop(body)
+        columns_loop(body, 0, length)
 
     handed = []
     along_a = {}
@@ -343,29 +354,36 @@
             far_a[db, half] = send(da, db, half, ring_a(side))
         hand(da, db, half)
 
-    weights(0, master, direction, master_out)
-    pass_on((0, 0), (0, 1))
+    for half in (0, 1):
+        weights(0, master, direction, master_out, half * HALF, HALF)
+        along_a[half, (0, half)] = send(0, 0, half, ring_a(half))
+    for side in (0, 1):
+        along_a[side, (0, 1 - side)] = send(0, 0, 1 - side, ring_a(side))
     hand(0, 0, 0)
     hand(0, 0, 1)
-    all_of(ahead_weight, 'weight', ahead_sem.at[0]).wait_recv()
-    all_of(ahead_step, 'step', ahead_sem.at[1]).wait_recv()
+    along_b = [send(0, 0, 1 - side, ring_b(side)) for side in (0, 1)]
+    all_of(ahead_weight.at[0], 'weight', ahead_sem.at[0]).wait_recv()
+    all_of(ahead_step.at[0], 'step', ahead_sem.at[1]).wait_recv()
     for side in (0, 1):
         db = 3 - 2 * side
-        weights(db, ahead_weight.at[side], ahead_step.at[side])
+        weights(db, ahead_weight.at[side], ahead_step.at[side], None, side * HALF, HALF)
         far_b[side] = send(0, db, side, ring_b(side))
     pass_on((3, 0), (1, 1))
+    hand(0, 3, 0)
+    hand(0, 1, 1)
+    for side in (0, 1):
+        arrived(side, 0, side)
+    for side in (0, 1):
+        along_b[side].wait_recv()
     pass_on((1, 0), (3, 1))
-    for half in (0, 1):
-        hand(0, 3, half)
-        hand(0, 1, 1 - half)
-    for side in (0, 1):
-        arrived(side, 0, side)
+    hand(0, 1, 0)
+    hand(0, 3, 1)
     for side in (0, 1):
         far_b[side].wait_recv()
     pass_on((2, 0), (2, 1))
     hand(0, 2, 0)
     hand(0, 2, 1)
-    for ref, group in ((relay_raw, 'raw'), (pair_raw, 'pair'), (early, 'early'), (late, 'late'), (mid, 'mid'), (end, 'end'), (ahead_weight, 'weight'), (ahead_step, 'step')):
+    for ref, group in ((relay_raw, 'raw'), (pair_raw, 'pair'), (early, 'early'), (late, 'late'), (mid, 'mid'), (end, 'end'), (ahead_weight.at[0], 'weight'), (ahead_step.at[0], 'step')):
         all_of(ref, group).wait_send()
     for copy in sum_sent:
         copy.wait_send()

time: 83.4 us -> 82.6 us (level)
  no operation moved by 1% of the time
where the time goes in v7:
time: 82.6 us; the launch traced here: 82.5 us
  Pallas kernels  81.9 us (99%)
    pallas_call x1, Pallas kernels, device_step(): pl.pallas_call(lamb_kernel, name='lamb_step', out_shape=(pltpu.VMEM((TILE...  78.6 us
    pallas_call x1, Pallas kernels, device_step(): pl.pallas_call(write_kernel, name='write_out', out_shape=tuple((pltpu.HBM...  3.33 us

profile of v7, /device:TPU:1, one launch (start us, length us, event | category | flops | bytes accessed | tf_op | source)
XLA Modules:
  0.0 82.5 jit_solution(620676906205708577)
XLA Ops:
  0.6 78.6 %lamb_step.1 = (bf16[3,8,147456]{2,1,0:T(8,128)(2,1)S(1)}, f32[3,8,4608]{2,1,0:T(8,128)S(1)}, f32[3,8,4608]{2,1,0:T(8,128)S(1)}, f32[3,8,4608]{2,1,0:T(8,128)S(1)}) custom-call(bf16[3,8,147456]{2,1,0:T(8,128)(2,1)} %bitcast.8, f32[3,8,4608]{2,1,0:T(8,128)} %bitcast.9, f32[3,8,4608]{2,1,0:T(8,128)} %bitcast.10, f32[3,8,4608]{2,1,0:T(8,128)} %bitcast.11), custom_call_target="tpu_custom_call" | custom-call | tf_op jit(solution)/shard_map/lamb_step/pallas_call | solution.py:436
  79.2 3.3 %write_out.1 = (bf16[3,8,147456]{2,1,0:T(8,128)(2,1)}, f32[3,8,4608]{2,1,0:T(8,128)}, f32[3,8,4608]{2,1,0:T(8,128)}, f32[3,8,4608]{2,1,0:T(8,128)}) custom-call(bf16[3,8,147456]{2,1,0:T(8,128)(2,1)S(1)} %get-tuple-element.12.params, f32[3,8,4608]{2,1,0:T(8,128)S(1)} %get-tuple-element.13.master, f32[3,8,4608]{2,1,0:T(8,128)S(1)} %get-tuple-element.14.one, ...), custom_call_target="tpu_custom_call" | custom-call | tf_op jit(solution)/shard_map/write_out/pallas_call | solution.py:476
